TPU v7x, 512 devices: a whole 4x4x16 slice. The times are simulated.
512 devices in a mesh: row: 16 (over z), col: 32 (over y, x, core).
Axes of the slice: x: 4, y: 4, z: 16, core: 2. Of those that a mesh axis runs over, the one named last changes fastest.
Arguments:
- momentum: float32 [8192, 26624], P('row', 'col'), may hold values from -6 to 6
- gradient: bfloat16 [8192, 26624], P('row', 'col'), may hold values from -150 to 150
- q_basis: bfloat16 [26624, 512], P('col', 'row'), may hold values from -0.0390625 to 0.0390625
Outputs:
- momentum_next: float32 [8192, 26624], P('row', 'col')
- p_basis: float32 [8192, 512], P(('row', 'col'))
- q_next: float32 [26624, 512], P('col', 'row')
All inputs are finite; a program needn't handle non-finite values.
Results may differ from a plain program's by a relative error of at most 0.0065.
Values may be sent and summed in bfloat16 or wider, within the bound.
A program may use at most 64 MiB of HBM per device.

v0:
```python
import jax
import jax.numpy as jnp
from jax import lax
from jax.sharding import Mesh
from jax.sharding import PartitionSpec as P

COL = ("col_0", "col_1", "col_2")
ROW_COL = ("row", "col_0", "col_1", "col_2")


def rows_for(lines, count):
    spare = -len(lines) % count
    return jnp.pad(lines, [(0, spare)] + [(0, 0)] * (lines.ndim - 1))


def from_everyone(shard, axis):
    copies = jnp.broadcast_to(shard, (lax.axis_size(axis), *shard.shape))
    return lax.all_to_all(copies, axis, split_axis=0, concat_axis=0, tiled=True)


def in_order(blocks, dim):
    blocks = jnp.moveaxis(blocks, 0, dim)
    lengths = blocks.shape
    return blocks.reshape(*lengths[:dim], lengths[dim] * lengths[dim + 1], *lengths[dim + 2 :])


def whole_of(shard, axes, dim):
    far, near = axes
    first = from_everyone(shard, far)
    blocks = jnp.swapaxes(from_everyone(first, near), 0, 1)
    return in_order(blocks.reshape(-1, *shard.shape), dim)


def in_blocks(shard, dim, count):
    before, after = (shard.shape[:dim], shard.shape[dim + 1 :])
    return jnp.moveaxis(shard.reshape(*before, count, -1, *after), dim, 0)


def sum_at_owner(shard, axis, dim):
    blocks = in_blocks(shard, dim, lax.axis_size(axis))
    arrived = lax.all_to_all(blocks, axis, split_axis=0, concat_axis=0, tiled=True)
    return arrived.sum(axis=0)


def sum_in_two_steps(shard, axes, dim):
    far, near = axes
    own = sum_at_owner(in_blocks(shard, dim, lax.axis_size(far)), near, dim + 1)
    return jnp.sum(lax.all_to_all(own, far, 0, 0, tiled=True), axis=0)


def nested_sum(shard, axes):
    lines = shard.reshape(-1, shard.shape[-1])
    padded = rows_for(lines, lax.axis_size(axes[0]) * lax.axis_size(axes[1]))
    whole = whole_of(sum_in_two_steps(padded, axes, 0), axes, 0)
    return lax.slice_in_dim(whole, 0, len(lines)).reshape(shard.shape)


def collect(shard, axis, dim):
    return in_order(from_everyone(shard, axis), dim)


def sum_by_parts(shard, axes):
    lines = shard.reshape(-1, shard.shape[-1])
    own = sum_at_owner(rows_for(lines, lax.axis_size(axes)), axes, 0)
    whole = collect(own, axes, 0)
    return whole[: len(lines)].reshape(shard.shape)


def over_copies(shard, axis):
    everything = from_everyone(shard, axis)
    return jnp.sum(everything, axis=0)


def body(momentum, gradient, q_basis):
    buffer = momentum + gradient.astype(jnp.float32)
    buffer_low = buffer.astype(jnp.bfloat16)
    power_part = jnp.dot(
        buffer_low,
        lax.all_gather(q_basis, "row", axis=1, tiled=True),
        preferred_element_type=jnp.float32,
    )
    row_share = buffer.shape[0] // lax.axis_size(COL)
    col_index = lax.axis_index(COL)
    power = nested_sum(power_part, (("col_0", "col_1"), "col_2"))
    local_gram = jnp.dot(power.T, power, precision=lax.Precision.HIGHEST)
    gram = sum_by_parts(local_gram, "row")
    lower = jnp.linalg.cholesky(gram)
    p_full = jax.scipy.linalg.solve_triangular(lower, power.T, lower=True).T
    p_low = p_full.astype(jnp.bfloat16)
    p_out = lax.dynamic_slice_in_dim(p_full, col_index * row_share, row_share, 0)
    right_part = jnp.einsum("ic,ir->cr", buffer_low, p_low, preferred_element_type=jnp.float32)
    right_cols = sum_at_owner(right_part, "row", 1)
    sums = over_copies(jnp.sum(right_cols * right_cols, axis=0), COL)
    q_next = right_cols / jnp.sqrt(sums + 1e-06)
    right_low = collect(right_cols.astype(jnp.bfloat16), "row", 1)
    update = jnp.einsum("ir,cr->ic", p_low, right_low, preferred_element_type=jnp.float32)
    return (buffer - 0.1 * update, p_out, q_next)


def solution(mesh):
    finer = Mesh(
        mesh.devices.reshape(mesh.shape["row"], 4, 4, 2), ("row", "col_0", "col_1", "col_2")
    )
    placed = (P("row", COL), P("row", COL), P(COL, "row"))
    return jax.shard_map(
        body,
        mesh=finer,
        in_specs=placed,
        out_specs=(P("row", COL), P(ROW_COL, None), P(COL, "row")),
        check_vma=False,
    )
```

profile of v0, /device:TPU:24, one launch (start us, length us, event | category | flops | bytes accessed | tf_op | source)
XLA Modules:
  0.0 509.6 jit_solution(14376004369528525037)
XLA Ops:
  0.6 40.9 %all_gather.3 = bf16[832,512]{0,1:T(8,128)(2,1)S(1)} all-gather(bf16[832,32]{0,1:T(8,128)(2,1)} %param.5), channel_id=1, replica_groups=mesh['row'=16,'col_0'=4,'col_1'=4,'col_2'=2] {'row'}, dimensions={1}, use_global_device_ids=true | all-gather | bytes 905216 | tf_op jit(solution)/shard_map/all_gather | solution.py:79
  41.6 2.5 fusion.35
  44.2 4.6 all_to_all.46
  48.8 16.5 %all_to_all.47 = f32[16,16,512]{2,1,0:T(8,128)S(1)} all-to-all(f32[16,16,512]{2,1,0:T(8,128)S(1)} %reduce_sum.54), channel_id=1, replica_groups=mesh['row'=16,'col_0'=4,'col_1'=4,'col_2'=2] {'col_0','col_1'}, dimensions={0} | all-to-all | bytes 1048576 | tf_op jit(solution)/shard_map/all_to_all | solution.py:48
  65.5 14.0 %all_to_all.48 = f32[16,16,512]{2,1,0:T(8,128)S(1)} all-to-all(f32[16,16,512]{2,1,0:T(8,128)S(1)} %broadcast_in_dim.18), channel_id=1, replica_groups=mesh['row'=16,'col_0'=4,'col_1'=4,'col_2'=2] {'col_0','col_1'}, dimensions={0} | all-to-all | bytes 1048576 | tf_op jit(solution)/shard_map/all_to_all | solution.py:18
  79.4 0.1 broadcast_in_dim.19
  79.6 4.6 all_to_all.49
  84.2 0.3 copy.34
  84.6 1.8 fusion.38
  86.4 58.3 %all_to_all.50 = f32[16,32,512]{2,1,0:T(8,128)S(1)} all-to-all(f32[16,32,512]{2,1,0:T(8,128)S(1)} %fusion.38), channel_id=1, replica_groups=mesh['row'=16,'col_0'=4,'col_1'=4,'col_2'=2] {'row'}, dimensions={0} | all-to-all | bytes 2097152 | tf_op jit(solution)/shard_map/all_to_all | solution.py:41
  144.8 1.1 broadcast_in_dim.20
  145.9 6.5 %all-to-all-start.5 = ((f32[16,32,512]{2,1,0:T(8,128)}), f32[16,32,512]{2,1,0:T(8,128)S(1)}, u32[]{:S(2)}, u32[]{:S(2)}) async-start(f32[16,32,512]{2,1,0:T(8,128)} %broadcast_in_dim.20), calls=%async_computation.5 | async-start | bytes 2097152 | tf_op jit(solution)/shard_map/all_to_all | solution.py:18
  152.4 49.9 %all-to-all-done.5 = f32[16,32,512]{2,1,0:T(8,128)S(1)} async-done(((f32[16,32,512]{2,1,0:T(8,128)}), f32[16,32,512]{2,1,0:T(8,128)S(1)}, u32[]{:S(2)}, u32[]{:S(2)}) %all-to-all-start.5) | async-done | bytes 1048608 | tf_op jit(solution)/shard_map/all_to_all | solution.py:18
  202.3 0.3 copy.35
  202.7 0.2 fusion.1
  202.9 1.0 copy-done.5
  203.9 11.7 %cholesky.104 = f32[128,128]{1,0:T(8,128)S(1)} custom-call(f32[128,128]{1,0:T(8,128)S(1)} %cholesky.266), custom_call_target="Cholesky" | custom-call | tf_op jit(solution)/shard_map/jit(cholesky)/cholesky | solution.py:87
  215.6 0.1 cholesky.224
  215.8 9.8 %custom-call.31 = f32[1,128,128]{1,2,0:T(8,128)S(1)} custom-call(f32[1,128,128]{2,1,0:T(8,128)S(1)} %get-tuple-element.47), custom_call_target="InvertDiagBlocksLowerTriangular" | custom-call | tf_op jit(solution)/shard_map/jit(cholesky)/cholesky | solution.py:87
  225.6 1.2 constant_dynamic-update-slice_fusion.3
  226.8 1.3 convolution_subtract_fusion.3
  228.1 11.7 %cholesky.217 = f32[128,128]{1,0:T(8,128)S(1)} custom-call(f32[128,128]{1,0:T(8,128)S(1)} %cholesky.270), custom_call_target="Cholesky" | custom-call | tf_op jit(solution)/shard_map/jit(cholesky)/cholesky | solution.py:87
  239.9 10.0 %custom-call.32 = f32[1,128,128]{1,2,0:T(8,128)S(1)} custom-call(f32[1,128,128]{2,1,0:T(8,128)S(1)} %get-tuple-element.44), custom_call_target="InvertDiagBlocksLowerTriangular" | custom-call | tf_op jit(solution)/shard_map/jit(cholesky)/cholesky | solution.py:87
  249.9 0.3 convolution_dynamic-update-slice_fusion
  250.1 1.3 convolution_subtract_fusion.4
  251.4 11.7 %cholesky.238 = f32[128,128]{1,0:T(8,128)S(1)} custom-call(f32[128,128]{1,0:T(8,128)S(1)} %cholesky.275), custom_call_target="Cholesky" | custom-call | tf_op jit(solution)/shard_map/jit(cholesky)/cholesky | solution.py:87
  263.2 9.8 %custom-call.33 = f32[1,128,128]{1,2,0:T(8,128)S(1)} custom-call(f32[1,128,128]{2,1,0:T(8,128)S(1)} %get-tuple-element.41), custom_call_target="InvertDiagBlocksLowerTriangular" | custom-call | tf_op jit(solution)/shard_map/jit(cholesky)/cholesky | solution.py:87
  273.0 0.2 convolution_dynamic-update-slice_fusion.1
  273.2 1.2 convolution_subtract_fusion.5
  274.5 11.7 %cholesky.255 = f32[128,128]{1,0:T(8,128)S(1)} custom-call(f32[128,128]{1,0:T(8,128)S(1)} %convolution_subtract_fusion.5), custom_call_target="Cholesky" | custom-call | tf_op jit(solution)/shard_map/jit(cholesky)/cholesky | solution.py:87
  286.2 0.7 compare_reduce_fusion.1
  286.9 0.6 compare_reduce_fusion
  287.5 0.6 compare_reduce_fusion.2
  290.7 0.4 select_select_fusion
  291.1 8.0 %while.1 = (s32[]{:T(128)}, f32[512,512]{1,0:T(8,128)S(1)}, s32[4,2]{0,1:T(2,128)S(1)}, f32[4,128,128]{2,1,0:T(8,128)S(1)}, s32[]{:T(128)}) while((s32[]{:T(128)}, f32[512,512]{1,0:T(8,128)S(1)}, s32[4,2]{0,1:T(2,128)S(1)}, f32[4,128,128]{2,1,0:T(8,128)S(1)}, s32[]{:T(128)}) %tuple.37), condition=%wide.while_cond, body=%wide.while_body.sunk | while | flops 2 | bytes 131189 | solution.py:88
  291.2 0.5 fusion.49
  291.7 1.4 bitcast_dynamic-update-slice_fusion.2
  293.2 0.5 fusion.49
  293.7 1.4 bitcast_dynamic-update-slice_fusion.2
  295.2 0.5 fusion.49
  295.7 1.4 bitcast_dynamic-update-slice_fusion.2
  297.2 0.5 fusion.49
  297.7 1.4 bitcast_dynamic-update-slice_fusion.2
  299.2 39.3 %custom-call.34 = f32[4,128,128]{1,2,0:T(8,128)S(1)} custom-call(f32[4,128,128]{2,1,0:T(8,128)S(1)} %get-tuple-element.10), custom_call_target="InvertDiagBlocksLowerTriangular" | custom-call | tf_op jit(solution)/shard_map/jit(_solve_triangular)/triangular_solve | solution.py:88
  338.5 0.4 fusion.10
  338.9 0.6 convolution_subtract_fusion.1
  339.6 0.4 fusion.26
  340.0 2.1 convolution_subtract_fusion
  342.1 1.3 fusion.24
  343.3 2.4 convolution_subtract_fusion.2
  345.7 1.3 fusion.23
  347.0 0.8 fusion.14
  347.8 94.1 %all_to_all.51 = f32[16,832,32]{1,2,0:T(8,128)} all-to-all(f32[16,832,32]{1,2,0:T(8,128)S(1)} %bitcast.81), channel_id=1, replica_groups=mesh['row'=16,'col_0'=4,'col_1'=4,'col_2'=2] {'row'}, dimensions={0} | all-to-all | bytes 3407872 | tf_op jit(solution)/shard_map/all_to_all | solution.py:41
  442.0 1.6 reduce_sum.57
  443.6 0.1 multiply_reduce_fusion
  443.7 10.9 %all_to_all.52 = f32[32,1,32]{2,1,0:T(1,128)S(1)} all-to-all(f32[32,1,32]{2,1,0:T(1,128)S(1)} %broadcast_in_dim.22), channel_id=1, replica_groups=mesh['row'=16,'col_0'=4,'col_1'=4,'col_2'=2] {'col_0','col_1','col_2'}, dimensions={0} | all-to-all | bytes 8192 | tf_op jit(solution)/shard_map/all_to_all | solution.py:18
  454.6 0.7 broadcast_divide_fusion
  455.4 1.0 broadcast_in_dim.21
  456.4 5.5 %all-to-all-start.7 = ((bf16[16,832,32]{1,2,0:T(8,128)(2,1)}), bf16[16,832,32]{1,2,0:T(8,128)(2,1)}, u32[]{:S(2)}, u32[]{:S(2)}) async-start(bf16[16,832,32]{1,2,0:T(8,128)(2,1)} %broadcast_in_dim.21), calls=%async_computation.7 | async-start | bytes 1835008 | tf_op jit(solution)/shard_map/all_to_all | solution.py:18
  461.9 1.1 pad_maximum_fusion
  463.0 0.8 dynamic-slice_bitcast_fusion
  463.9 1.7 copy.41
  465.5 40.5 %all-to-all-done.7 = bf16[16,832,32]{1,2,0:T(8,128)(2,1)} async-done(((bf16[16,832,32]{1,2,0:T(8,128)(2,1)}), bf16[16,832,32]{1,2,0:T(8,128)(2,1)}, u32[]{:S(2)}, u32[]{:S(2)}) %all-to-all-start.7) | async-done | bytes 852000 | tf_op jit(solution)/shard_map/all_to_all | solution.py:18
  506.1 3.1 multiply_subtract_fusion
  (36 shorter events, 1.0 us)
Async XLA Ops:
  145.9 56.4 %all-to-all-start.5 = ((f32[16,32,512]{2,1,0:T(8,128)}), f32[16,32,512]{2,1,0:T(8,128)S(1)}, u32[]{:S(2)}, u32[]{:S(2)}) async-start(f32[16,32,512]{2,1,0:T(8,128)} %broadcast_in_dim.20), calls=%async_computation.5 | async-start | bytes 2097152 | tf_op jit(solution)/shard_map/all_to_all | solution.py:18
  202.9 1.0 copy-start.5
  299.1 40.4 %copy-start.4 = (f32[512,512]{1,0:T(8,128)}, f32[512,512]{1,0:T(8,128)S(1)}, u32[]{:S(2)}) copy-start(f32[512,512]{1,0:T(8,128)S(1)} %get-tuple-element.97) | copy-start | bytes 3145732
  338.5 1.1 copy-start.6
  340.0 7.0 %copy-start = (f32[512,832]{0,1:T(8,128)S(1)}, f32[512,832]{0,1:T(8,128)}, u32[]{:S(2)}) copy-start(f32[512,832]{0,1:T(8,128)} %param.3) | copy-start | bytes 5111812
  340.0 7.0 %copy-start.1 = (bf16[512,832]{0,1:T(8,128)(2,1)S(1)}, bf16[512,832]{0,1:T(8,128)(2,1)}, u32[]{:S(2)}) copy-start(bf16[512,832]{0,1:T(8,128)(2,1)} %param.4) | copy-start | bytes 2555908
  347.0 0.8 copy-start.3
  456.4 49.7 %all-to-all-start.7 = ((bf16[16,832,32]{1,2,0:T(8,128)(2,1)}), bf16[16,832,32]{1,2,0:T(8,128)(2,1)}, u32[]{:S(2)}, u32[]{:S(2)}) async-start(bf16[16,832,32]{1,2,0:T(8,128)(2,1)} %broadcast_in_dim.21), calls=%async_computation.7 | async-start | bytes 1835008 | tf_op jit(solution)/shard_map/all_to_all | solution.py:18
  461.9 44.2 %copy-start.2 = (bf16[512,832]{0,1:T(8,128)(2,1)S(1)}, bf16[512,832]{0,1:T(8,128)(2,1)}, u32[]{:S(2)}) copy-start(bf16[512,832]{0,1:T(8,128)(2,1)} %param.4) | copy-start | bytes 2555908
where the time goes:
time: 517 us; the launch traced here: 510 us
  blocking collectives  244 us (47%)
  other arithmetic  122 us (24%)
  waiting for transfers between devices  90.4 us (17%)
  matrix products  22.1 us (4%)
  local copies, waits for them, and re-layouts  14.7 us (3%)
  starting transfers between devices  12 us (2%)
    all_to_all x3, blocking collectives, sum_at_owner(): lax.all_to_all(blocks, axis, split_axis=0, concat_axis=0, tiled=True)  157 us
    all_to_all x2, waiting for transfers between devices, from_everyone(): return lax.all_to_all(copies, axis, split_axis=0, concat_axis=0, tiled=True)  90.4 us
    another operation x14, other arithmetic, body(): lower = jnp.linalg.cholesky(gram)  78.6 us
    all_gather x1, blocking collectives, body(): lax.all_gather(q_basis, 'row', axis=1, tiled=True)  40.9 us
    another operation x4, other arithmetic, body(): p_full = jax.scipy.linalg.solve_triangular(lower, power.T, lower=True).T  40.8 us
    all_to_all x3, blocking collectives, from_everyone(): return lax.all_to_all(copies, axis, split_axis=0, concat_axis=0, tiled=True)  29.5 us
    all_to_all x1, blocking collectives, sum_in_two_steps(): return jnp.sum(lax.all_to_all(own, far, 0, 0, tiled=True), axis=0)  16.5 us
    all_to_all x2, starting transfers between devices, from_everyone(): return lax.all_to_all(copies, axis, split_axis=0, concat_axis=0, tiled=True)  12 us
  transfers between devices with their start and end apart: 2, of which 2 were waited for; matrix products, arithmetic and copies ran while one was open for 1% of the time, Pallas kernels for 0%

commit v1 on v0

v1 whole, which is shorter than its diff:
```python
import jax
import jax.numpy as jnp
from jax import lax
from jax.experimental import pallas as pl
from jax.experimental.pallas import tpu as pltpu
from jax.sharding import PartitionSpec as P

HI = lax.Precision.HIGHEST
MESH = pl.DeviceIdType.MESH
F32, BF16 = jnp.float32, jnp.bfloat16
NB = 128
DMA = pltpu.SemaphoreType.DMA
NT = (((1,), (1,)), ((), ()))
TN = (((0,), (0,)), ((), ()))


def send(src, dst, send_sem, recv_sem, **where):
    copy = pltpu.make_async_remote_copy(
        src_ref=src, dst_ref=dst, send_sem=send_sem, recv_sem=recv_sem, device_id=where, device_id_type=MESH
    )
    copy.start()
    return copy


def drain(view, sem):
    pltpu.make_async_copy(view, view, sem).wait()


def greet(z, c, nz, nc, near):
    barrier = pltpu.get_barrier_semaphore()
    if near:
        for step in (1, nz - 1):
            pl.semaphore_signal(barrier, inc=1, device_id={"row": lax.rem(z + step, nz)}, device_id_type=MESH)
    else:
        @pl.loop(1, nz)
        def _(j):
            pl.semaphore_signal(barrier, inc=1, device_id={"row": lax.rem(z + j, nz)}, device_id_type=MESH)

    @pl.loop(1, nc)
    def _(j):
        pl.semaphore_signal(barrier, inc=1, device_id={"col": lax.rem(c + j, nc)}, device_id_type=MESH)

    def met():
        pl.semaphore_wait(barrier, (2 if near else nz - 1) + nc - 1)

    return met


class Ring:
    def __init__(self, held, send_sems, recv_sems, z, nz):
        self.held, self.ss, self.rs = held, send_sems, recv_sems
        self.nz, self.half = nz, nz // 2
        self.ways = (lax.rem(z + 1, nz), lax.rem(z + nz - 1, nz))
        self.sent, self.got = [], set()

    def arrived(self, slot, chunk):
        if slot != 0 and (slot, chunk) not in self.got:
            self.got.add((slot, chunk))
            drain(self.held.at[slot, chunk], self.rs.at[slot, chunk])

    def step(self, t):
        for chunk in (0, 1):
            for way in (0, 1):
                if t == self.half and chunk != way:
                    continue
                src, dst = (t - 1, t) if way == 0 else ((self.nz - t + 1) % self.nz, self.nz - t)
                self.arrived(src, chunk)
                self.sent.append(send(
                    self.held.at[src, chunk], self.held.at[dst, chunk],
                    self.ss.at[way, t - 1, chunk], self.rs.at[dst, chunk], row=self.ways[way]))

    def slot_arrived(self, slot):
        for chunk in (0, 1):
            self.arrived(slot, chunk)

    def finish(self):
        for copy in self.sent:
            copy.wait_send()


def power_kernel(
    nz, nc, mom_ref, grad_ref, q_ref, w_ref, g_ref,
    blow, held, parts, came, shares, gpart, gcame, grow, gall,
    q_ss, q_rs, c_ss, c_rs, a_ss, a_rs, d_ss, d_rs, z_ss, z_rs, y_ss, y_rs, g_ss, g_rs, e_ss, e_rs,
):
    z, c = lax.axis_index("row"), lax.axis_index("col")
    chip, core = lax.div(c, 2), lax.rem(c, 2)
    partner = chip * 2 + 1 - core
    chips, half = nc // 2, nz // 2
    met = greet(z, c, nz, nc, False)
    blow[...] = (mom_ref[...] + grad_ref[...].astype(F32)).astype(BF16)
    rows = blow.shape[1]
    lanes = rows // 128
    wide = q_ref.shape[0]
    for chunk in (0, 1):
        held[0, chunk] = q_ref[chunk * (wide // 2):(chunk + 1) * (wide // 2), :]
    met()
    ring = Ring(held, q_ss, q_rs, z, nz)
    sides = [(t, (nz - t) % nz if t else half) for t in range(half)]

    def multiply(p):
        for slot in sides[p]:
            ring.slot_arrived(slot)
        lhs = jnp.concatenate([held[slot].reshape(wide, -1) for slot in sides[p]], axis=0)
        prod = jnp.dot(lhs, blow[...], preferred_element_type=F32)
        for side in (0, 1):
            for piece in range(chips):
                s, l = piece // lanes, piece % lanes
                parts[p, side, piece] = prod[side * wide + 8 * s:side * wide + 8 * s + 8, 128 * l:128 * l + 128]
        came[p, c] = parts[p, core, chip]

        @pl.loop(1, nc)
        def _(j):
            to = lax.rem(c + j, nc)
            send(parts.at[p, lax.rem(to, 2), lax.div(to, 2)], came.at[p, c], c_ss.at[p], c_rs.at[p], col=to)

    def add_up(p):
        drain(came.at[p, pl.ds(0, nc - 1)], c_rs.at[p])
        shares[p, core, chip] = came[p].sum(axis=0)

        @pl.loop(1, chips)
        def _(j):
            to = lax.rem(chip + j, chips) * 2 + core
            mine = shares.at[p, core, chip]
            send(mine, mine, a_ss.at[p], a_rs.at[p], col=to)

    def cross(p):
        drain(shares.at[p, core, pl.ds(0, chips - 1)], a_rs.at[p])
        view = shares.at[p, core]
        send(view, view, d_ss.at[p], d_rs.at[p], col=partner)

    order = list(range(1, half)) + [0]
    ring.step(1)
    for i in range(half + 4):
        if i + 2 <= half:
            ring.step(i + 2)
        if i < half:
            multiply(order[i])
        if 0 <= i - 2 < half:
            add_up(order[i - 2])
        if 0 <= i - 4 < half:
            cross(order[i - 4])
    for p in range(half):
        drain(shares.at[p, core], d_rs.at[p])
    for p in range(half):
        for side in (0, 1):
            at = lax.rem(z + nz - sides[p][side], nz) * wide
            for piece in range(chips):
                s, l = piece // lanes, piece % lanes
                w_ref[pl.ds(pl.multiple_of(at + 8 * s, 8), 8), 128 * l:128 * l + 128] = shares[p, side, piece]

    share = w_ref.shape[0] // nc
    mine = w_ref[pl.ds(pl.multiple_of(c * share, share), share), :]
    prod = lax.dot_general(mine, w_ref[...], NT, precision=HI, preferred_element_type=F32)
    glanes = prod.shape[1] // 128
    tall = share * glanes // nz
    for piece in range(nz):
        s, l = piece // glanes, piece % glanes
        gpart[piece] = prod[tall * s:tall * (s + 1), 128 * l:128 * l + 128]
    gcame[z] = gpart[z]

    @pl.loop(1, nz)
    def _(j):
        to = lax.rem(z + j, nz)
        send(gpart.at[to], gcame.at[z], z_ss, z_rs, row=to)

    drain(gcame.at[pl.ds(0, nz - 1)], z_rs)
    grow[z] = gcame[...].sum(axis=0)

    @pl.loop(1, nz)
    def _(j):
        to = lax.rem(z + j, nz)
        send(grow.at[z], grow.at[z], y_ss, y_rs, row=to)

    drain(grow.at[pl.ds(0, nz - 1)], y_rs)
    gall[core, chip] = grow[...]

    @pl.loop(1, chips)
    def _(j):
        to = lax.rem(chip + j, chips) * 2 + core
        mine = gall.at[core, chip]
        send(mine, mine, g_ss, g_rs, col=to)

    drain(gall.at[core, pl.ds(0, chips - 1)], g_rs)
    across = send(gall.at[core], gall.at[core], e_ss, e_rs, col=partner)
    ring.finish()
    for p in range(half):
        drain(came.at[p, pl.ds(0, nc - 1)], c_ss.at[p])
        drain(shares.at[p, core, pl.ds(0, chips - 1)], a_ss.at[p])
        drain(shares.at[p, core], d_ss.at[p])
    drain(gcame.at[pl.ds(0, nz - 1)], z_ss)
    drain(grow.at[pl.ds(0, nz - 1)], y_ss)
    drain(gall.at[core, pl.ds(0, chips - 1)], g_ss)
    across.wait()
    for other in range(nc):
        for piece in range(nz):
            s, l = piece // glanes, piece % glanes
            top = other * share + tall * s
            g_ref[top:top + tall, 128 * l:128 * l + 128] = gall[other % 2, other // 2, piece]


def power_and_gram(mom, grad, q, nz, nc):
    cols, rows = mom.shape
    wide = q.shape[0]
    rank, half, chips = wide * nz, nz // 2, nc // 2
    share = rank // nc
    tall = share * (rank // 128) // nz
    whole = pl.BlockSpec(memory_space=pltpu.VMEM)
    return pl.pallas_call(
        lambda *refs: power_kernel(nz, nc, *refs),
        out_shape=(jax.ShapeDtypeStruct((rank, rows), F32), jax.ShapeDtypeStruct((rank, rank), F32)),
        in_specs=[whole] * 3,
        out_specs=(whole, whole),
        scratch_shapes=[
            pltpu.VMEM((cols, rows), BF16),
            pltpu.VMEM((nz, 2, wide // 2, cols), BF16),
            pltpu.VMEM((half, 2, chips, 8, 128), F32),
            pltpu.VMEM((half, nc, 8, 128), F32),
            pltpu.VMEM((half, 2, chips, 8, 128), F32),
            pltpu.VMEM((nz, tall, 128), F32),
            pltpu.VMEM((nz, tall, 128), F32),
            pltpu.VMEM((nz, tall, 128), F32),
            pltpu.VMEM((2, chips, nz, tall, 128), F32),
            DMA((2, half, 2)), DMA((nz, 2)),
            DMA((half,)), DMA((half,)), DMA((half,)), DMA((half,)), DMA((half,)), DMA((half,)),
            DMA, DMA, DMA, DMA, DMA, DMA, DMA, DMA,
        ],
        compiler_params=pltpu.CompilerParams(
            collective_id=0, has_side_effects=True, vmem_limit_bytes=40 * 1024 * 1024),
        name="power_and_gram",
    )(mom, grad, q)


def sub_bcast(x, j):
    return jnp.broadcast_to(x[j:j + 1, :], x.shape)


def lane_bcast(x, j):
    return jnp.broadcast_to(x[:, j:j + 1], x.shape)


def diag_inverse(d_ref, inv_ref):
    n = NB // 8
    row = lax.broadcasted_iota(jnp.int32, (8, NB), 0)
    lane = lax.broadcasted_iota(jnp.int32, (8, NB), 1)
    for g in range(n):
        inv_ref[8 * g:8 * g + 8, :] = jnp.where(row + 8 * g == lane, 1.0, 0.0).astype(jnp.float32)
    for s in range(n):
        rd = d_ref[8 * s:8 * s + 8, :]
        ri = inv_ref[8 * s:8 * s + 8, :]
        c = [lane_bcast(rd, 8 * s + k) for k in range(8)]
        u = {}
        scale = []
        ud = []
        ui = []
        for j in range(8):
            rs = lax.rsqrt(sub_bcast(c[j], j))
            scale.append(rs)
            lj = jnp.where(row > j, c[j] * rs, 0.0)
            for k in range(j + 1, 8):
                u[j, k] = sub_bcast(c[k], j) * rs
                c[k] = c[k] - lj * u[j, k]
            ud.append(sub_bcast(rd, j) * rs)
            ui.append(sub_bcast(ri, j) * rs)
            rd = rd - lj * ud[j]
            ri = ri - lj * ui[j]
        out = ui[7]
        for j in range(7):
            out = jnp.where(row == j, ui[j], out)
        inv_ref[8 * s:8 * s + 8, :] = out
        for g in range(s + 1, n):
            rd = d_ref[8 * g:8 * g + 8, :]
            ri = inv_ref[8 * g:8 * g + 8, :]
            c = [lane_bcast(rd, 8 * s + k) for k in range(8)]
            for j in range(8):
                lj = c[j] * scale[j]
                for k in range(j + 1, 8):
                    c[k] = c[k] - lj * u[j, k]
                rd = rd - lj * ud[j]
                ri = ri - lj * ui[j]
            d_ref[8 * g:8 * g + 8, :] = rd
            inv_ref[8 * g:8 * g + 8, :] = ri


def solve_kernel(g_ref, w_ref, low_ref, p_ref, a, d, inv, pt):
    rank = w_ref.shape[0]
    rows = w_ref.shape[1]
    blocks = rank // NB
    a[:, :rank] = g_ref[...]
    a[:, rank:] = w_ref[...]

    def step(b, carry):
        at = pl.multiple_of(b * NB, NB)
        d[...] = a[pl.ds(at, NB), pl.ds(at, NB)]
        diag_inverse(d, inv)
        for bb in range(blocks):
            @pl.when(b == bb)
            def _():
                lo, hi = bb * NB, (bb + 1) * NB
                y = jnp.dot(inv[...], a[lo:hi, hi:], precision=HI, preferred_element_type=jnp.float32)
                x = y[:, rank - hi:]
                a[lo:hi, rank:] = x
                if bb < blocks - 1:
                    ut = y[:, :rank - hi].T
                    a[hi:rank, hi:] = a[hi:rank, hi:] - jnp.dot(
                        ut, y, precision=HI, preferred_element_type=jnp.float32)
        return carry

    lax.fori_loop(0, blocks, step, 0)
    full = a[:, rank:]
    low_ref[...] = full.astype(jnp.bfloat16)
    pt[...] = full.T
    share = p_ref.shape[0]
    mine = lax.axis_index("col") * share
    p_ref[...] = pt[pl.ds(pl.multiple_of(mine, share), share), :]


def solve(gram, w, share):
    rank, rows = w.shape
    whole = pl.BlockSpec(memory_space=pltpu.VMEM)
    return pl.pallas_call(
        solve_kernel,
        out_shape=(jax.ShapeDtypeStruct((rank, rows), jnp.bfloat16), jax.ShapeDtypeStruct((share, rank), jnp.float32)),
        in_specs=[whole, whole],
        out_specs=(whole, whole),
        scratch_shapes=[
            pltpu.VMEM((rank, rank + rows), jnp.float32),
            pltpu.VMEM((NB, NB), jnp.float32),
            pltpu.VMEM((NB, NB), jnp.float32),
            pltpu.VMEM((rows, rank), jnp.float32),
        ],
        compiler_params=pltpu.CompilerParams(vmem_limit_bytes=40 * 1024 * 1024),
        name="solve",
    )(gram, w)


def right_kernel(
    nz, nc, mom_ref, grad_ref, p_ref, out_ref, q_ref,
    blow, part, stage, came, cols, held, turned, sums, sums_came,
    r_ss, r_rs, q_ss, q_rs, n_ss, n_rs,
):
    z, c = lax.axis_index("row"), lax.axis_index("col")
    half = nz // 2
    met = greet(z, c, nz, nc, True)
    blow[...] = (mom_ref[...] + grad_ref[...].astype(F32)).astype(BF16)
    wide = q_ref.shape[0]
    thin = wide // 2
    prod = lax.dot_general(p_ref[...], blow[...], NT, preferred_element_type=F32)
    for block in range(nz):
        for chunk in (0, 1):
            at = block * wide + chunk * thin
            part[block, chunk] = prod[at:at + thin, :]
    met()
    ways = (lax.rem(z + nz - 1, nz), lax.rem(z + 1, nz))
    sent = []
    for s in range(half):
        for chunk in (0, 1):
            for way in (0, 1):
                first = int(chunk != way)
                if s < first:
                    continue
                far = half - s
                target = lax.rem(z + (nz - far if way == 0 else far), nz)
                value = part[target, chunk]
                if s > first:
                    drain(came.at[way, s - 1, chunk], r_rs.at[way, s - 1, chunk])
                    value = value + came[way, s - 1, chunk].astype(F32)
                stage[way, s, chunk] = value.astype(BF16)
                sent.append(send(
                    stage.at[way, s, chunk], came.at[way, s, chunk],
                    r_ss.at[way, s, chunk], r_rs.at[way, s, chunk], row=ways[way]))
    total = jnp.zeros((wide, 1), F32)
    both = []
    for chunk in (0, 1):
        value = part[z, chunk]
        for way in (0, 1):
            drain(came.at[way, half - 1, chunk], r_rs.at[way, half - 1, chunk])
            value = value + came[way, half - 1, chunk].astype(F32)
        cols[chunk] = value
        held[0, chunk] = value.astype(BF16)
    ring = Ring(held, q_ss, q_rs, z, nz)
    ring.step(1)
    value = cols[...].reshape(wide, -1)
    sums[...] = jnp.broadcast_to(jnp.sum(value * value, axis=1, keepdims=True), (wide, 128))
    sums_came[c] = sums[...]

    @pl.loop(1, nc)
    def _(j):
        send(sums, sums_came.at[c], n_ss, n_rs, col=lax.rem(c + j, nc))

    for slot in range(nz):
        at = lax.rem(z + nz - slot, nz) * wide
        turned[wide * slot:wide * (slot + 1), :] = p_ref[pl.ds(pl.multiple_of(at, wide), wide), :]
    for t in range(2, half + 1):
        ring.step(t)
        if t == half - 1:
            drain(sums_came.at[pl.ds(0, nc - 1)], n_rs)
            norms = jnp.sqrt(jnp.sum(sums_came[...], axis=0)[:, :1] + 1e-06)
            q_ref[...] = value / norms
    for slot in range(nz):
        ring.slot_arrived(slot)
    right = held[...].reshape(nz * wide, -1)
    update = lax.dot_general(right, turned[...], TN, preferred_element_type=F32)
    out_ref[...] = (mom_ref[...] + grad_ref[...].astype(F32)) - 0.1 * update
    for copy in sent:
        copy.wait_send()
    ring.finish()
    drain(sums_came.at[pl.ds(0, nc - 1)], n_ss)


def right_and_update(mom, grad, p, nz, nc):
    cols, rows = mom.shape
    rank = p.shape[0]
    half, wide = nz // 2, rank // nz
    thin = wide // 2
    whole = pl.BlockSpec(memory_space=pltpu.VMEM)
    return pl.pallas_call(
        lambda *refs: right_kernel(nz, nc, *refs),
        out_shape=(jax.ShapeDtypeStruct((cols, rows), F32), jax.ShapeDtypeStruct((wide, cols), F32)),
        in_specs=[whole] * 3,
        out_specs=(whole, whole),
        scratch_shapes=[
            pltpu.VMEM((cols, rows), BF16),
            pltpu.VMEM((nz, 2, thin, cols), F32),
            pltpu.VMEM((2, half, 2, thin, cols), BF16),
            pltpu.VMEM((2, half, 2, thin, cols), BF16),
            pltpu.VMEM((2, thin, cols), F32),
            pltpu.VMEM((nz, 2, thin, cols), BF16),
            pltpu.VMEM((rank, rows), BF16),
            pltpu.VMEM((wide, 128), F32),
            pltpu.VMEM((nc, wide, 128), F32),
            DMA((2, half, 2)), DMA((2, half, 2)), DMA((2, half, 2)), DMA((nz, 2)), DMA, DMA,
        ],
        compiler_params=pltpu.CompilerParams(
            collective_id=1, has_side_effects=True, vmem_limit_bytes=40 * 1024 * 1024),
        name="right_and_update",
    )(mom, grad, p)


def solution(mesh):
    nz, nc = mesh.shape["row"], mesh.shape["col"]

    def body(momentum, gradient, q_basis):
        mom, grad, q = momentum.T, gradient.T, q_basis.T
        w, gram = power_and_gram(mom, grad, q, nz, nc)
        p_low, p_out = solve(gram, w, w.shape[1] // nc)
        mom_next, q_next = right_and_update(mom, grad, p_low, nz, nc)
        return mom_next.T, p_out, q_next.T

    placed = (P("row", "col"), P("row", "col"), P("col", "row"))
    return jax.shard_map(
        body, mesh=mesh, in_specs=placed, out_specs=(P("row", "col"), P(("row", "col"), None), P("col", "row")),
        check_vma=False,
    )
```

time: 517 us -> 164 us (0.32); the launches traced: 510 us -> 163 us
  blocking collectives: 244 us -> 0 us
  Pallas kernels: 0 us -> 158 us
  other arithmetic: 122 us -> 0 us
  waiting for transfers between devices: 90.4 us -> 0 us
  matrix products: 22.1 us -> 0 us
  starting transfers between devices: 12 us -> 0 us
  local copies, waits for them, and re-layouts: 14.7 us -> 5.27 us
    all_to_all x7 -> x0, blocking collectives: 203 us -> none  [the longest x3 157 us: sum_at_owner(): lax.all_to_all(blocks, axis, split_axis=0, concat_axis=0, tiled=True)]
    pallas_call x0 -> x3, Pallas kernels: none -> 158 us  [the longest x1 77.9 us: power_and_gram(): pl.pallas_call(lambda *refs: power_kernel(nz, nc, *refs), out_shape=(jax....]
    another operation x18 -> x0, other arithmetic: 119 us -> none  [the longest x14 78.6 us: body(): lower = jnp.linalg.cholesky(gram)]
    all_to_all x2 -> x0, waiting for transfers between devices: 90.4 us -> none  [from_everyone(): return lax.all_to_all(copies, axis, split_axis=0, concat_axis=0, tiled=True)]
    all_gather x1 -> x0, blocking collectives: 40.9 us -> none  [body(): lax.all_gather(q_basis, 'row', axis=1, tiled=True)]
    another operation x13 -> x0, matrix products: 13.9 us -> none  [the longest x7 8.43 us: body(): p_full = jax.scipy.linalg.solve_triangular(lower, power.T, lower=True).T]
    all_to_all x2 -> x0, starting transfers between devices: 12 us -> none  [from_everyone(): return lax.all_to_all(copies, axis, split_axis=0, concat_axis=0, tiled=True)]
    dot_general x4 -> x0, matrix products: 8.2 us -> none  [the longest x1 3.12 us: body(): jnp.einsum('ir,cr->ic', p_low, right_low, preferred_element_type=jnp.floa...]
  transfers between devices with their start and end apart: 2 -> 0, of which waited for: 2 -> 0; matrix products, arithmetic and copies ran while one was open for 1% -> 0% of each run, Pallas kernels for 0% -> 0%
where the time goes in v1:
time: 164 us; the launch traced here: 163 us
  Pallas kernels  158 us (96%)
  local copies, waits for them, and re-layouts  5.27 us (3%)
    pallas_call x1, Pallas kernels, power_and_gram(): pl.pallas_call(lambda *refs: power_kernel(nz, nc, *refs), out_shape=(jax....  77.9 us
    pallas_call x1, Pallas kernels, right_and_update(): pl.pallas_call(lambda *refs: right_kernel(nz, nc, *refs), out_shape=(jax....  58.6 us
    pallas_call x1, Pallas kernels, solve(): pl.pallas_call(solve_kernel, out_shape=(jax.ShapeDtypeStruct((rank, rows)...  21 us
    unnamed x12, local copies, waits for them, and re-layouts  5.27 us

profile of v1, /device:TPU:24, one launch (start us, length us, event | category | flops | bytes accessed | tf_op | source)
XLA Modules:
  0.0 163.4 jit_solution(9525880789957387574)
XLA Ops:
  0.6 0.0 copy-start
  0.6 1.4 copy-done
  2.1 0.0 copy-start.2
  2.1 1.2 copy-done.2
  3.2 0.0 copy-start.4
  3.2 0.8 copy-done.4
  4.1 0.0 copy-start.3
  4.1 77.9 %power_and_gram.1 = (f32[512,512]{1,0:T(8,128)S(1)}, f32[512,512]{1,0:T(8,128)S(1)}) custom-call(f32[832,512]{1,0:T(8,128)S(1)} %bitcast.5, bf16[832,512]{1,0:T(8,128)(2,1)S(1)} %bitcast.7, bf16[32,832]{1,0:T(8,128)(2,1)S(1)} %bitcast.11), custom_call_target="tpu_custom_call" | custom-call | tf_op jit(solution)/shard_map/power_and_gram/pallas_call | solution.py:209
  82.0 0.0 copy-start.1
  82.0 21.0 %solve.1 = (bf16[512,512]{1,0:T(8,128)(2,1)S(1)}, f32[16,512]{1,0:T(8,128)}) custom-call(f32[512,512]{1,0:T(8,128)S(1)} %get-tuple-element.9.g_ref, f32[512,512]{1,0:T(8,128)S(1)} %get-tuple-element.10.w_ref), custom_call_target="tpu_custom_call" | custom-call | tf_op jit(solution)/shard_map/solve/pallas_call | solution.py:321
  103.0 0.0 copy-done.3
  103.0 0.0 copy-done.1
  103.0 58.6 %right_and_update.1 = (f32[832,512]{1,0:T(8,128)S(1)}, f32[32,832]{1,0:T(8,128)S(1)}) custom-call(f32[832,512]{1,0:T(8,128)S(1)} %bitcast.6, bf16[832,512]{1,0:T(8,128)(2,1)S(1)} %bitcast.8, bf16[512,512]{1,0:T(8,128)(2,1)S(1)} %get-tuple-element.11.refs_2_), custom_call_target="tpu_custom_call" | custom-call | tf_op jit(solution)/shard_map/right_and_update/pallas_call | solution.py:417
  161.6 1.2 copy.8
  162.8 0.6 copy.9
Async XLA Ops:
  0.6 1.5 copy-start
  2.1 1.2 copy-start.2
  3.2 0.8 copy-start.4
  4.1 98.9 %copy-start.3 = (bf16[512,832]{0,1:T(8,128)(2,1)S(1)}, bf16[512,832]{0,1:T(8,128)(2,1)}, u32[]{:S(2)}) copy-start(bf16[512,832]{0,1:T(8,128)(2,1)} %param.4) | copy-start | bytes 2555908
  82.0 21.0 %copy-start.1 = (f32[512,832]{0,1:T(8,128)S(1)}, f32[512,832]{0,1:T(8,128)}, u32[]{:S(2)}) copy-start(f32[512,832]{0,1:T(8,128)} %param.3) | copy-start | bytes 5111812

commit v2 on v1

--- a/solution.py
+++ b/solution.py
@@ -26,22 +26,18 @@
     pltpu.make_async_copy(view, view, sem).wait()
 
 
-def greet(z, c, nz, nc, near):
+def greet(z, c, nz, nc):
     barrier = pltpu.get_barrier_semaphore()
-    if near:
-        for step in (1, nz - 1):
-            pl.semaphore_signal(barrier, inc=1, device_id={"row": lax.rem(z + step, nz)}, device_id_type=MESH)
-    else:
-        @pl.loop(1, nz)
-        def _(j):
-            pl.semaphore_signal(barrier, inc=1, device_id={"row": lax.rem(z + j, nz)}, device_id_type=MESH)
+    near = (1, 2, nz - 2, nz - 1)
+    for step in near:
+        pl.semaphore_signal(barrier, inc=1, device_id={"row": lax.rem(z + step, nz)}, device_id_type=MESH)
 
     @pl.loop(1, nc)
     def _(j):
         pl.semaphore_signal(barrier, inc=1, device_id={"col": lax.rem(c + j, nc)}, device_id_type=MESH)
 
     def met():
-        pl.semaphore_wait(barrier, (2 if near else nz - 1) + nc - 1)
+        pl.semaphore_wait(barrier, len(near) + nc - 1)
 
     return met
 
@@ -50,7 +46,8 @@
     def __init__(self, held, send_sems, recv_sems, z, nz):
         self.held, self.ss, self.rs = held, send_sems, recv_sems
         self.nz, self.half = nz, nz // 2
-        self.ways = (lax.rem(z + 1, nz), lax.rem(z + nz - 1, nz))
+        self.rounds = self.half // 2
+        self.to = [[lax.rem(z + step, nz) for step in (hops, nz - hops)] for hops in (1, 2)]
         self.sent, self.got = [], set()
 
     def arrived(self, slot, chunk):
@@ -58,20 +55,24 @@
             self.got.add((slot, chunk))
             drain(self.held.at[slot, chunk], self.rs.at[slot, chunk])
 
-    def step(self, t):
-        for chunk in (0, 1):
-            for way in (0, 1):
-                if t == self.half and chunk != way:
-                    continue
-                src, dst = (t - 1, t) if way == 0 else ((self.nz - t + 1) % self.nz, self.nz - t)
-                self.arrived(src, chunk)
-                self.sent.append(send(
-                    self.held.at[src, chunk], self.held.at[dst, chunk],
-                    self.ss.at[way, t - 1, chunk], self.rs.at[dst, chunk], row=self.ways[way]))
-
-    def slot_arrived(self, slot):
-        for chunk in (0, 1):
-            self.arrived(slot, chunk)
+    def slots_arrived(self, *slots):
+        for slot in slots:
+            for chunk in (0, 1):
+                self.arrived(slot % self.nz, chunk)
+
+    def round(self, r):
+        for hops in (2, 1):
+            for chunk in (0, 1):
+                for way in (0, 1):
+                    src, dst = 2 * r, 2 * r + hops
+                    if dst == self.half and chunk != way:
+                        continue
+                    if way:
+                        src, dst = (self.nz - src) % self.nz, self.nz - dst
+                    self.arrived(src, chunk)
+                    self.sent.append(send(
+                        self.held.at[src, chunk], self.held.at[dst, chunk],
+                        self.ss.at[way, r, hops - 1, chunk], self.rs.at[dst, chunk], row=self.to[hops - 1][way]))
 
     def finish(self):
         for copy in self.sent:
@@ -79,30 +80,40 @@
 
 
 def power_kernel(
-    nz, nc, mom_ref, grad_ref, q_ref, w_ref, g_ref,
-    blow, held, parts, came, shares, gpart, gcame, grow, gall,
-    q_ss, q_rs, c_ss, c_rs, a_ss, a_rs, d_ss, d_rs, z_ss, z_rs, y_ss, y_rs, g_ss, g_rs, e_ss, e_rs,
+    nz, nc, mom_ref, grad_ref, q_ref, w_out, g_ref,
+    w_ref, mom, grad, blow, held, parts, came, shares, gpart, gcame, grow, gall,
+    q_ss, q_rs, c_ss, c_rs, a_ss, a_rs, d_ss, d_rs, z_ss, z_rs, y_ss, y_rs, g_ss, g_rs, e_ss, e_rs, i_s,
 ):
     z, c = lax.axis_index("row"), lax.axis_index("col")
     chip, core = lax.div(c, 2), lax.rem(c, 2)
     partner = chip * 2 + 1 - core
     chips, half = nc // 2, nz // 2
-    met = greet(z, c, nz, nc, False)
-    blow[...] = (mom_ref[...] + grad_ref[...].astype(F32)).astype(BF16)
+    wide = q_ref.shape[0]
+    thin = wide // 2
+    copies = [pltpu.make_async_copy(q_ref.at[pl.ds(thin * chunk, thin)], held.at[0, chunk], i_s.at[chunk]) for chunk in (0, 1)]
+    loads = [pltpu.make_async_copy(grad_ref, grad, i_s.at[2]), pltpu.make_async_copy(mom_ref, mom, i_s.at[3])]
+    for copy in copies:
+        copy.start()
+    met = greet(z, c, nz, nc)
+    for copy in loads:
+        copy.start()
     rows = blow.shape[1]
     lanes = rows // 128
-    wide = q_ref.shape[0]
-    for chunk in (0, 1):
-        held[0, chunk] = q_ref[chunk * (wide // 2):(chunk + 1) * (wide // 2), :]
+    for copy in copies:
+        copy.wait()
     met()
     ring = Ring(held, q_ss, q_rs, z, nz)
     sides = [(t, (nz - t) % nz if t else half) for t in range(half)]
 
-    def multiply(p):
-        for slot in sides[p]:
-            ring.slot_arrived(slot)
-        lhs = jnp.concatenate([held[slot].reshape(wide, -1) for slot in sides[p]], axis=0)
+    def multiply(*pairs):
+        slots = [slot for p in pairs for slot in sides[p]]
+        ring.slots_arrived(*slots)
+        lhs = jnp.concatenate([held[slot].reshape(wide, -1) for slot in slots], axis=0)
         prod = jnp.dot(lhs, blow[...], preferred_element_type=F32)
+        for i, p in enumerate(pairs):
+            pass_on(p, prod[2 * wide * i:2 * wide * (i + 1)])
+
+    def pass_on(p, prod):
         for side in (0, 1):
             for piece in range(chips):
                 s, l = piece // lanes, piece % lanes
@@ -118,30 +129,43 @@
         drain(came.at[p, pl.ds(0, nc - 1)], c_rs.at[p])
         shares[p, core, chip] = came[p].sum(axis=0)
 
-        @pl.loop(1, chips)
-        def _(j):
-            to = lax.rem(chip + j, chips) * 2 + core
-            mine = shares.at[p, core, chip]
-            send(mine, mine, a_ss.at[p], a_rs.at[p], col=to)
+        mine = shares.at[p, core, chip]
+        if p in late:
+            @pl.loop(1, nc)
+            def _(j):
+                send(mine, mine, a_ss.at[p], a_rs.at[p], col=lax.rem(c + j, nc))
+        else:
+            @pl.loop(1, chips)
+            def _(j):
+                send(mine, mine, a_ss.at[p], a_rs.at[p], col=lax.rem(chip + j, chips) * 2 + core)
 
     def cross(p):
         drain(shares.at[p, core, pl.ds(0, chips - 1)], a_rs.at[p])
         view = shares.at[p, core]
         send(view, view, d_ss.at[p], d_rs.at[p], col=partner)
 
-    order = list(range(1, half)) + [0]
-    ring.step(1)
-    for i in range(half + 4):
-        if i + 2 <= half:
-            ring.step(i + 2)
-        if i < half:
-            multiply(order[i])
-        if 0 <= i - 2 < half:
-            add_up(order[i - 2])
-        if 0 <= i - 4 < half:
-            cross(order[i - 4])
+    late = (half - 1, 0)
+    groups = [(2 * r - 1, 2 * r) for r in range(1, ring.rounds)] + [late]
+    ring.round(0)
+    for copy in loads:
+        copy.wait()
+    blow[...] = (mom[...] + grad[...].astype(F32)).astype(BF16)
+    for i in range(len(groups) + 2):
+        if i + 1 < ring.rounds:
+            ring.round(i + 1)
+        if i < len(groups):
+            multiply(*groups[i])
+        if 1 <= i <= len(groups):
+            for p in groups[i - 1]:
+                add_up(p)
+        if 2 <= i <= len(groups):
+            for p in groups[i - 2]:
+                cross(p)
     for p in range(half):
-        drain(shares.at[p, core], d_rs.at[p])
+        if p in late:
+            drain(came.at[p, pl.ds(0, nc - 1)], a_rs.at[p])
+        else:
+            drain(shares.at[p, core], d_rs.at[p])
     for p in range(half):
         for side in (0, 1):
             at = lax.rem(z + nz - sides[p][side], nz) * wide
@@ -149,6 +173,8 @@
                 s, l = piece // lanes, piece % lanes
                 w_ref[pl.ds(pl.multiple_of(at + 8 * s, 8), 8), 128 * l:128 * l + 128] = shares[p, side, piece]
 
+    w_copy = pltpu.make_async_copy(w_ref, w_out, i_s.at[0])
+    w_copy.start()
     share = w_ref.shape[0] // nc
     mine = w_ref[pl.ds(pl.multiple_of(c * share, share), share), :]
     prod = lax.dot_general(mine, w_ref[...], NT, precision=HI, preferred_element_type=F32)
@@ -183,11 +209,15 @@
 
     drain(gall.at[core, pl.ds(0, chips - 1)], g_rs)
     across = send(gall.at[core], gall.at[core], e_ss, e_rs, col=partner)
+    w_copy.wait()
     ring.finish()
     for p in range(half):
         drain(came.at[p, pl.ds(0, nc - 1)], c_ss.at[p])
-        drain(shares.at[p, core, pl.ds(0, chips - 1)], a_ss.at[p])
-        drain(shares.at[p, core], d_ss.at[p])
+        if p in late:
+            drain(came.at[p, pl.ds(0, nc - 1)], a_ss.at[p])
+        else:
+            drain(shares.at[p, core, pl.ds(0, chips - 1)], a_ss.at[p])
+            drain(shares.at[p, core], d_ss.at[p])
     drain(gcame.at[pl.ds(0, nz - 1)], z_ss)
     drain(grow.at[pl.ds(0, nz - 1)], y_ss)
     drain(gall.at[core, pl.ds(0, chips - 1)], g_ss)
@@ -206,12 +236,16 @@
     share = rank // nc
     tall = share * (rank // 128) // nz
     whole = pl.BlockSpec(memory_space=pltpu.VMEM)
+    away = pl.BlockSpec(memory_space=pltpu.HBM)
     return pl.pallas_call(
         lambda *refs: power_kernel(nz, nc, *refs),
         out_shape=(jax.ShapeDtypeStruct((rank, rows), F32), jax.ShapeDtypeStruct((rank, rank), F32)),
-        in_specs=[whole] * 3,
-        out_specs=(whole, whole),
+        in_specs=[away] * 3,
+        out_specs=(away, whole),
         scratch_shapes=[
+            pltpu.VMEM((rank, rows), F32),
+            pltpu.VMEM((cols, rows), F32),
+            pltpu.VMEM((cols, rows), BF16),
             pltpu.VMEM((cols, rows), BF16),
             pltpu.VMEM((nz, 2, wide // 2, cols), BF16),
             pltpu.VMEM((half, 2, chips, 8, 128), F32),
@@ -221,12 +255,12 @@
             pltpu.VMEM((nz, tall, 128), F32),
             pltpu.VMEM((nz, tall, 128), F32),
             pltpu.VMEM((2, chips, nz, tall, 128), F32),
-            DMA((2, half, 2)), DMA((nz, 2)),
+            DMA((2, half // 2, 2, 2)), DMA((nz, 2)),
             DMA((half,)), DMA((half,)), DMA((half,)), DMA((half,)), DMA((half,)), DMA((half,)),
-            DMA, DMA, DMA, DMA, DMA, DMA, DMA, DMA,
+            DMA, DMA, DMA, DMA, DMA, DMA, DMA, DMA, DMA((4,)),
         ],
         compiler_params=pltpu.CompilerParams(
-            collective_id=0, has_side_effects=True, vmem_limit_bytes=40 * 1024 * 1024),
+            collective_id=0, has_side_effects=True, vmem_limit_bytes=67043328),
         name="power_and_gram",
     )(mom, grad, q)
 
@@ -336,12 +370,12 @@
 
 def right_kernel(
     nz, nc, mom_ref, grad_ref, p_ref, out_ref, q_ref,
-    blow, part, stage, came, cols, held, turned, sums, sums_came,
-    r_ss, r_rs, q_ss, q_rs, n_ss, n_rs,
+    blow, part, leaf, leaf_came, stem, stem_came, cols, held, turned, sums, sums_came,
+    l_ss, l_rs, r_ss, r_rs, q_ss, q_rs, n_ss, n_rs,
 ):
     z, c = lax.axis_index("row"), lax.axis_index("col")
     half = nz // 2
-    met = greet(z, c, nz, nc, True)
+    met = greet(z, c, nz, nc)
     blow[...] = (mom_ref[...] + grad_ref[...].astype(F32)).astype(BF16)
     wide = q_ref.shape[0]
     thin = wide // 2
@@ -351,35 +385,45 @@
             at = block * wide + chunk * thin
             part[block, chunk] = prod[at:at + thin, :]
     met()
-    ways = (lax.rem(z + nz - 1, nz), lax.rem(z + 1, nz))
+    to = [[lax.rem(z + step, nz) for step in (nz - hops, hops)] for hops in (1, 2)]
     sent = []
-    for s in range(half):
+
+    def own(way, far, chunk):
+        return part[lax.rem(z + (far if way else nz - far), nz), chunk]
+
+    def inbound(came, sems, way, k, chunk):
+        drain(came.at[way, k, chunk], sems.at[way, k, chunk])
+        return came[way, k, chunk].astype(F32)
+
+    def outbound(value, held_out, came, send_sems, recv_sems, way, k, chunk, hops):
+        held_out[way, k, chunk] = value.astype(BF16)
+        sent.append(send(
+            held_out.at[way, k, chunk], came.at[way, k, chunk],
+            send_sems.at[way, k, chunk], recv_sems.at[way, k, chunk], row=to[hops - 1][way]))
+
+    for far in range(half, 0, -2):
+        k = far // 2
         for chunk in (0, 1):
             for way in (0, 1):
-                first = int(chunk != way)
-                if s < first:
+                if far == half and chunk != way:
                     continue
-                far = half - s
-                target = lax.rem(z + (nz - far if way == 0 else far), nz)
-                value = part[target, chunk]
-                if s > first:
-                    drain(came.at[way, s - 1, chunk], r_rs.at[way, s - 1, chunk])
-                    value = value + came[way, s - 1, chunk].astype(F32)
-                stage[way, s, chunk] = value.astype(BF16)
-                sent.append(send(
-                    stage.at[way, s, chunk], came.at[way, s, chunk],
-                    r_ss.at[way, s, chunk], r_rs.at[way, s, chunk], row=ways[way]))
-    total = jnp.zeros((wide, 1), F32)
-    both = []
+                value = own(way, far, chunk)
+                if far < half:
+                    value = value + inbound(leaf_came, l_rs, way, k, chunk)
+                if far < half - 2 or (far < half and chunk == way):
+                    value = value + inbound(stem_came, r_rs, way, k, chunk)
+                outbound(value, stem, stem_came, r_ss, r_rs, way, k - 1, chunk, 2)
+        for chunk in (0, 1):
+            for way in (0, 1):
+                outbound(own(way, far - 1, chunk), leaf, leaf_came, l_ss, l_rs, way, k - 1, chunk, 1)
     for chunk in (0, 1):
         value = part[z, chunk]
         for way in (0, 1):
-            drain(came.at[way, half - 1, chunk], r_rs.at[way, half - 1, chunk])
-            value = value + came[way, half - 1, chunk].astype(F32)
+            value = value + inbound(leaf_came, l_rs, way, 0, chunk) + inbound(stem_came, r_rs, way, 0, chunk)
         cols[chunk] = value
         held[0, chunk] = value.astype(BF16)
     ring = Ring(held, q_ss, q_rs, z, nz)
-    ring.step(1)
+    ring.round(0)
     value = cols[...].reshape(wide, -1)
     sums[...] = jnp.broadcast_to(jnp.sum(value * value, axis=1, keepdims=True), (wide, 128))
     sums_came[c] = sums[...]
@@ -391,14 +435,13 @@
     for slot in range(nz):
         at = lax.rem(z + nz - slot, nz) * wide
         turned[wide * slot:wide * (slot + 1), :] = p_ref[pl.ds(pl.multiple_of(at, wide), wide), :]
-    for t in range(2, half + 1):
-        ring.step(t)
-        if t == half - 1:
+    for r in range(1, ring.rounds):
+        ring.round(r)
+        if r == ring.rounds - 1:
             drain(sums_came.at[pl.ds(0, nc - 1)], n_rs)
             norms = jnp.sqrt(jnp.sum(sums_came[...], axis=0)[:, :1] + 1e-06)
             q_ref[...] = value / norms
-    for slot in range(nz):
-        ring.slot_arrived(slot)
+    ring.slots_arrived(*range(nz))
     right = held[...].reshape(nz * wide, -1)
     update = lax.dot_general(right, turned[...], TN, preferred_element_type=F32)
     out_ref[...] = (mom_ref[...] + grad_ref[...].astype(F32)) - 0.1 * update
@@ -422,14 +465,17 @@
         scratch_shapes=[
             pltpu.VMEM((cols, rows), BF16),
             pltpu.VMEM((nz, 2, thin, cols), F32),
-            pltpu.VMEM((2, half, 2, thin, cols), BF16),
-            pltpu.VMEM((2, half, 2, thin, cols), BF16),
+            pltpu.VMEM((2, half // 2, 2, thin, cols), BF16),
+            pltpu.VMEM((2, half // 2, 2, thin, cols), BF16),
+            pltpu.VMEM((2, half // 2, 2, thin, cols), BF16),
+            pltpu.VMEM((2, half // 2, 2, thin, cols), BF16),
             pltpu.VMEM((2, thin, cols), F32),
             pltpu.VMEM((nz, 2, thin, cols), BF16),
             pltpu.VMEM((rank, rows), BF16),
             pltpu.VMEM((wide, 128), F32),
             pltpu.VMEM((nc, wide, 128), F32),
-            DMA((2, half, 2)), DMA((2, half, 2)), DMA((2, half, 2)), DMA((nz, 2)), DMA, DMA,
+            DMA((2, half // 2, 2)), DMA((2, half // 2, 2)), DMA((2, half // 2, 2)), DMA((2, half // 2, 2)),
+            DMA((2, half // 2, 2, 2)), DMA((nz, 2)), DMA, DMA,
         ],
         compiler_params=pltpu.CompilerParams(
             collective_id=1, has_side_effects=True, vmem_limit_bytes=40 * 1024 * 1024),

time: 164 us -> 144 us (0.88); the launches traced: 163 us -> 141 us
  Pallas kernels: 158 us -> 135 us
    pallas_call x1, Pallas kernels: 58.6 us -> 44 us  [right_and_update(): pl.pallas_call(lambda *refs: right_kernel(nz, nc, *refs), out_shape=(jax....]
    pallas_call x1, Pallas kernels: 77.9 us -> 70.2 us  [power_and_gram(): pl.pallas_call(lambda *refs: power_kernel(nz, nc, *refs), out_shape=(jax....]
    unnamed x12 -> x10, local copies, waits for them, and re-layouts: 5.27 us -> 5.56 us
where the time goes in v2:
time: 144 us; the launch traced here: 141 us
  Pallas kernels  135 us (94%)
  local copies, waits for them, and re-layouts  5.56 us (4%)
    pallas_call x1, Pallas kernels, power_and_gram(): pl.pallas_call(lambda *refs: power_kernel(nz, nc, *refs), out_shape=(jax....  70.2 us
    pallas_call x1, Pallas kernels, right_and_update(): pl.pallas_call(lambda *refs: right_kernel(nz, nc, *refs), out_shape=(jax....  44 us
    pallas_call x1, Pallas kernels, solve(): pl.pallas_call(solve_kernel, out_shape=(jax.ShapeDtypeStruct((rank, rows)...  21 us
    unnamed x10, local copies, waits for them, and re-layouts  5.56 us

profile of v2, /device:TPU:24, one launch (start us, length us, event | category | flops | bytes accessed | tf_op | source)
XLA Modules:
  0.0 141.5 jit_solution(8038889391532975514)
XLA Ops:
  0.6 70.2 %power_and_gram.1 = (f32[512,512]{1,0:T(8,128)}, f32[512,512]{1,0:T(8,128)}) custom-call(f32[832,512]{1,0:T(8,128)} %bitcast.5, bf16[832,512]{1,0:T(8,128)(2,1)} %bitcast.7, bf16[32,832]{1,0:T(8,128)(2,1)} %bitcast.11), custom_call_target="tpu_custom_call" | custom-call | tf_op jit(solution)/shard_map/power_and_gram/pallas_call | solution.py:240
  70.9 0.0 copy-start
  70.9 0.0 copy-start.2
  70.9 1.3 copy-done.2
  72.2 0.0 copy-start.3
  72.2 1.2 copy-done.3
  73.5 21.0 %solve.1 = (bf16[512,512]{1,0:T(8,128)(2,1)S(1)}, f32[16,512]{1,0:T(8,128)}) custom-call(f32[512,512]{1,0:T(8,128)S(1)} %copy-done.3, f32[512,512]{1,0:T(8,128)S(1)} %copy-done.2), custom_call_target="tpu_custom_call" | custom-call | tf_op jit(solution)/shard_map/solve/pallas_call | solution.py:355
  94.4 0.0 copy-done
  94.5 0.0 copy-start.1
  94.5 1.2 copy-done.1
  95.6 44.0 %right_and_update.1 = (f32[832,512]{1,0:T(8,128)S(1)}, f32[32,832]{1,0:T(8,128)S(1)}) custom-call(f32[832,512]{1,0:T(8,128)S(1)} %bitcast.6, bf16[832,512]{1,0:T(8,128)(2,1)S(1)} %bitcast.8, bf16[512,512]{1,0:T(8,128)(2,1)S(1)} %get-tuple-element.11.refs_2_), custom_call_target="tpu_custom_call" | custom-call | tf_op jit(solution)/shard_map/right_and_update/pallas_call | solution.py:460
  139.6 1.2 copy.8
  140.8 0.6 copy.9
Async XLA Ops:
  70.9 23.6 %copy-start = (f32[512,832]{0,1:T(8,128)S(1)}, f32[512,832]{0,1:T(8,128)}, u32[]{:S(2)}) copy-start(f32[512,832]{0,1:T(8,128)} %param.3) | copy-start | bytes 5111812
  70.9 1.4 copy-start.2
  72.2 1.2 copy-start.3
  94.5 1.2 copy-start.1

commit v3 on v0

v3 whole, which is shorter than its diff:
```python
from types import SimpleNamespace

import jax
import jax.numpy as jnp
from jax import lax
from jax.experimental import pallas as pl
from jax.experimental.pallas import tpu as pltpu
from jax.sharding import PartitionSpec as P

HI = lax.Precision.HIGHEST
MESH = pl.DeviceIdType.MESH
F32, BF16 = jnp.float32, jnp.bfloat16
NB = 128
DMA = pltpu.SemaphoreType.DMA
NT = (((1,), (1,)), ((), ()))
TN = (((0,), (0,)), ((), ()))


def send(src, dst, send_sem, recv_sem, **where):
    copy = pltpu.make_async_remote_copy(
        src_ref=src, dst_ref=dst, send_sem=send_sem, recv_sem=recv_sem, device_id=where, device_id_type=MESH
    )
    copy.start()
    return copy


def drain(view, sem):
    pltpu.make_async_copy(view, view, sem).wait()


def greet(z, c, nz, nc):
    barrier = pltpu.get_barrier_semaphore()
    near = (1, 2, nz - 2, nz - 1)
    for step in near:
        pl.semaphore_signal(barrier, inc=1, device_id={"row": lax.rem(z + step, nz)}, device_id_type=MESH)

    @pl.loop(1, nc)
    def _(j):
        pl.semaphore_signal(barrier, inc=1, device_id={"col": lax.rem(c + j, nc)}, device_id_type=MESH)

    def met():
        pl.semaphore_wait(barrier, len(near) + nc - 1)

    return met


class Ring:
    def __init__(self, held, send_sems, recv_sems, z, nz):
        self.held, self.ss, self.rs = held, send_sems, recv_sems
        self.nz, self.half = nz, nz // 2
        self.rounds = self.half // 2
        self.to = [[lax.rem(z + step, nz) for step in (hops, nz - hops)] for hops in (1, 2)]
        self.sent, self.got = [], set()

    def arrived(self, slot, chunk):
        if slot != 0 and (slot, chunk) not in self.got:
            self.got.add((slot, chunk))
            drain(self.held.at[slot, chunk], self.rs.at[slot, chunk])

    def slots_arrived(self, *slots):
        for slot in slots:
            for chunk in (0, 1):
                self.arrived(slot % self.nz, chunk)

    def round(self, r):
        for hops in (2, 1):
            for chunk in (0, 1):
                for way in (0, 1):
                    src, dst = 2 * r, 2 * r + hops
                    if dst == self.half and chunk != way:
                        continue
                    if way:
                        src, dst = (self.nz - src) % self.nz, self.nz - dst
                    self.arrived(src, chunk)
                    self.sent.append(send(
                        self.held.at[src, chunk], self.held.at[dst, chunk],
                        self.ss.at[way, r, hops - 1, chunk], self.rs.at[dst, chunk], row=self.to[hops - 1][way]))

    def finish(self):
        for copy in self.sent:
            copy.wait_send()


def sub_bcast(x, j):
    return jnp.broadcast_to(x[j:j + 1, :], x.shape)


def lane_bcast(x, j):
    return jnp.broadcast_to(x[:, j:j + 1], x.shape)


def diag_inverse(d_ref, inv_ref):
    n = NB // 8
    row = lax.broadcasted_iota(jnp.int32, (8, NB), 0)
    lane = lax.broadcasted_iota(jnp.int32, (8, NB), 1)
    for g in range(n):
        inv_ref[8 * g:8 * g + 8, :] = jnp.where(row + 8 * g == lane, 1.0, 0.0).astype(jnp.float32)
    for s in range(n):
        rd = d_ref[8 * s:8 * s + 8, :]
        ri = inv_ref[8 * s:8 * s + 8, :]
        c = [lane_bcast(rd, 8 * s + k) for k in range(8)]
        u = {}
        scale = []
        ud = []
        ui = []
        for j in range(8):
            rs = lax.rsqrt(sub_bcast(c[j], j))
            scale.append(rs)
            lj = jnp.where(row > j, c[j] * rs, 0.0)
            for k in range(j + 1, 8):
                u[j, k] = sub_bcast(c[k], j) * rs
                c[k] = c[k] - lj * u[j, k]
            ud.append(sub_bcast(rd, j) * rs)
            ui.append(sub_bcast(ri, j) * rs)
            rd = rd - lj * ud[j]
            ri = ri - lj * ui[j]
        out = ui[7]
        for j in range(7):
            out = jnp.where(row == j, ui[j], out)
        inv_ref[8 * s:8 * s + 8, :] = out
        for g in range(s + 1, n):
            rd = d_ref[8 * g:8 * g + 8, :]
            ri = inv_ref[8 * g:8 * g + 8, :]
            c = [lane_bcast(rd, 8 * s + k) for k in range(8)]
            for j in range(8):
                lj = c[j] * scale[j]
                for k in range(j + 1, 8):
                    c[k] = c[k] - lj * u[j, k]
                rd = rd - lj * ud[j]
                ri = ri - lj * ui[j]
            d_ref[8 * g:8 * g + 8, :] = rd
            inv_ref[8 * g:8 * g + 8, :] = ri


def scratch_of(nz, nc, cols, rows, wide):
    rank, half, chips = wide * nz, nz // 2, nc // 2
    thin, quarter, hi = wide // 2, nz // 4, rank // 2
    tall = (rank // nc) * (rank // 128) // nz
    win = window_rows(cols, nz)
    vm = pltpu.VMEM
    return dict(
        mom=vm((cols, rows), F32), grad=vm((cols, rows), BF16), blow=vm((cols, rows), BF16),
        held=vm((nz, 2, thin, cols), BF16),
        parts=vm((half, 2, chips, 8, 128), F32), came=vm((half, nc, 8, 128), F32),
        shares=vm((half, 2, chips, 8, 128), F32), w=vm((rank, rows), F32),
        gpart=vm((nz, tall, 128), F32), gcame=vm((nz, tall, 128), F32), grow=vm((nz, tall, 128), F32),
        gall=vm((2, chips, nz, tall, 128), F32),
        a=vm((rank, 2 * rank), F32), d=vm((NB, NB), F32), inv=vm((NB, NB), F32),
        y=vm((2, cols, hi), F32),
        leaf_came=vm((2, quarter, 2, win, hi), F32), stem=vm((2, quarter, 2, win, hi), F32),
        stem_came=vm((2, quarter, 2, win, hi), F32), own=vm((2, win, hi), F32),
        right=vm((nz, 2, win, hi), BF16), r32=vm((cols, rank), F32),
        plow=vm((rank, rows), BF16), pt=vm((rows, rank), F32),
        sz=vm((nz, rank // 128, 128), F32), sx=vm((nc, rank // 128, 128), F32),
        q_ss=DMA((2, quarter, 2, 2)), q_rs=DMA((nz, 2)),
        c_ss=DMA((half,)), c_rs=DMA((half,)), a_ss=DMA((half,)), a_rs=DMA((half,)), d_ss=DMA((half,)), d_rs=DMA((half,)),
        z_ss=DMA, z_rs=DMA, y_ss=DMA, y_rs=DMA, g_ss=DMA, g_rs=DMA, e_ss=DMA, e_rs=DMA,
        l_ss=DMA((2, quarter, 2)), l_rs=DMA((2, quarter, 2)), r_ss=DMA((2, quarter, 2)), r_rs=DMA((2, quarter, 2)),
        p_ss=DMA((2, quarter, 2, 2)), p_rs=DMA((nz, 2)),
        n_ss=DMA, n_rs=DMA, m_ss=DMA, m_rs=DMA, i_s=DMA((4,)),
    )


def window_rows(cols, nz):
    return -(-(cols // nz) // 8) * 8


def window_start(i, cols, nz):
    return pl.multiple_of(lax.div(i * (cols // nz), 8) * 8, 8)


def split3(x):
    one = x.astype(BF16)
    rest = x - one.astype(F32)
    two = rest.astype(BF16)
    return one, two, (rest - two.astype(F32)).astype(BF16)


def kernel(nz, nc, mom_hbm, grad_hbm, q_hbm, m_out, p_out, q_out, s):
    z, c = lax.axis_index("row"), lax.axis_index("col")
    chip, core = lax.div(c, 2), lax.rem(c, 2)
    partner = chip * 2 + 1 - core
    chips, half = nc // 2, nz // 2
    wide = q_hbm.shape[0]
    thin = wide // 2
    cols, rows = s.blow.shape
    rank = wide * nz
    hi = rank // 2
    lanes = rows // 128

    def others(count):
        return pl.ds(0, count - 1)

    copies = [
        pltpu.make_async_copy(q_hbm.at[pl.ds(thin * chunk, thin)], s.held.at[0, chunk], s.i_s.at[chunk])
        for chunk in (0, 1)
    ]
    loads = [pltpu.make_async_copy(grad_hbm, s.grad, s.i_s.at[2]), pltpu.make_async_copy(mom_hbm, s.mom, s.i_s.at[3])]
    for copy in copies:
        copy.start()
    met = greet(z, c, nz, nc)
    for copy in loads:
        copy.start()
    for copy in copies:
        copy.wait()
    met()

    ring = Ring(s.held, s.q_ss, s.q_rs, z, nz)
    sides = [(t, (nz - t) % nz if t else half) for t in range(half)]
    late = (half - 1, 0)
    groups = [(2 * r - 1, 2 * r) for r in range(1, ring.rounds)] + [late]

    def multiply(*pairs):
        slots = [slot for p in pairs for slot in sides[p]]
        ring.slots_arrived(*slots)
        lhs = jnp.concatenate([s.held[slot].reshape(wide, -1) for slot in slots], axis=0)
        prod = jnp.dot(lhs, s.blow[...], preferred_element_type=F32)
        for i, p in enumerate(pairs):
            pass_on(p, prod[2 * wide * i:2 * wide * (i + 1)])

    def pass_on(p, prod):
        for side in (0, 1):
            for piece in range(chips):
                i, l = piece // lanes, piece % lanes
                s.parts[p, side, piece] = prod[side * wide + 8 * i:side * wide + 8 * i + 8, 128 * l:128 * l + 128]
        s.came[p, c] = s.parts[p, core, chip]

        @pl.loop(1, nc)
        def _(j):
            to = lax.rem(c + j, nc)
            send(s.parts.at[p, lax.rem(to, 2), lax.div(to, 2)], s.came.at[p, c], s.c_ss.at[p], s.c_rs.at[p], col=to)

    def add_up(p):
        drain(s.came.at[p, others(nc)], s.c_rs.at[p])
        s.shares[p, core, chip] = s.came[p].sum(axis=0)
        mine = s.shares.at[p, core, chip]
        if p in late:
            @pl.loop(1, nc)
            def _(j):
                send(mine, mine, s.a_ss.at[p], s.a_rs.at[p], col=lax.rem(c + j, nc))
        else:
            @pl.loop(1, chips)
            def _(j):
                send(mine, mine, s.a_ss.at[p], s.a_rs.at[p], col=lax.rem(chip + j, chips) * 2 + core)

    def cross(p):
        drain(s.shares.at[p, core, others(chips)], s.a_rs.at[p])
        view = s.shares.at[p, core]
        send(view, view, s.d_ss.at[p], s.d_rs.at[p], col=partner)

    ring.round(0)
    for copy in loads:
        copy.wait()
    s.blow[...] = (s.mom[...] + s.grad[...].astype(F32)).astype(BF16)
    for i in range(len(groups)):
        if i + 1 < ring.rounds:
            ring.round(i + 1)
        multiply(*groups[i])
        if i >= 2:
            for p in groups[i - 2]:
                add_up(p)
    for p in groups[-2]:
        add_up(p)
    for p in groups[0]:
        cross(p)
    for p in late:
        add_up(p)
    for group in groups[1:-1]:
        for p in group:
            cross(p)
    for p in range(half):
        if p in late:
            drain(s.came.at[p, others(nc)], s.a_rs.at[p])
        else:
            drain(s.shares.at[p, core], s.d_rs.at[p])
    for p in range(half):
        for side in (0, 1):
            at = lax.rem(z + nz - sides[p][side], nz) * wide
            for piece in range(chips):
                i, l = piece // lanes, piece % lanes
                s.w[pl.ds(pl.multiple_of(at + 8 * i, 8), 8), 128 * l:128 * l + 128] = s.shares[p, side, piece]

    share = rank // nc
    mine = s.w[pl.ds(pl.multiple_of(c * share, share), share), :]
    prod = lax.dot_general(mine, s.w[...], NT, precision=HI, preferred_element_type=F32)
    glanes = rank // 128
    tall = share * glanes // nz
    for piece in range(nz):
        i, l = piece // glanes, piece % glanes
        s.gpart[piece] = prod[tall * i:tall * (i + 1), 128 * l:128 * l + 128]
    s.gcame[z] = s.gpart[z]

    @pl.loop(1, nz)
    def _(j):
        to = lax.rem(z + j, nz)
        send(s.gpart.at[to], s.gcame.at[z], s.z_ss, s.z_rs, row=to)

    pieces = split3(s.w[...])
    for chunk in (0, 1):
        s.y[chunk] = sum(
            lax.dot_general(s.blow[...], piece[hi * chunk:hi * (chunk + 1)], NT, preferred_element_type=F32)
            for piece in reversed(pieces)
        )

    drain(s.gcame.at[others(nz)], s.z_rs)
    s.grow[z] = s.gcame[...].sum(axis=0)

    @pl.loop(1, nz)
    def _(j):
        send(s.grow.at[z], s.grow.at[z], s.y_ss, s.y_rs, row=lax.rem(z + j, nz))

    win = window_rows(cols, nz)
    to = [[lax.rem(z + step, nz) for step in (nz - hops, hops)] for hops in (1, 2)]

    def share_of(i, chunk):
        return s.y.at[chunk, pl.ds(window_start(i, cols, nz), win), :]

    def far_one(way, far):
        return lax.rem(z + (far if way else nz - far), nz)

    def inbound(came, sems, way, k, chunk):
        drain(came.at[way, k, chunk], sems.at[way, k, chunk])
        return came[way, k, chunk]

    def sum_round(far):
        k = far // 2
        for chunk in (0, 1):
            for way in (0, 1):
                if far == half and chunk != way:
                    continue
                value = share_of(far_one(way, far), chunk)[...]
                if far < half:
                    value = value + inbound(s.leaf_came, s.l_rs, way, k, chunk)
                if far < half - 2 or (far < half and chunk == way):
                    value = value + inbound(s.stem_came, s.r_rs, way, k, chunk)
                s.stem[way, k - 1, chunk] = value
                send(s.stem.at[way, k - 1, chunk], s.stem_came.at[way, k - 1, chunk],
                     s.r_ss.at[way, k - 1, chunk], s.r_rs.at[way, k - 1, chunk], row=to[1][way])
        for chunk in (0, 1):
            for way in (0, 1):
                send(share_of(far_one(way, far - 1), chunk), s.leaf_came.at[way, k - 1, chunk],
                     s.l_ss.at[way, k - 1, chunk], s.l_rs.at[way, k - 1, chunk], row=to[0][way])

    sum_round(half)
    drain(s.grow.at[others(nz)], s.y_rs)
    s.gall[core, chip] = s.grow[...]

    @pl.loop(1, chips)
    def _(j):
        mine = s.gall.at[core, chip]
        send(mine, mine, s.g_ss, s.g_rs, col=lax.rem(chip + j, chips) * 2 + core)

    row = lax.broadcasted_iota(jnp.int32, (NB, rank), 0)
    lane = lax.broadcasted_iota(jnp.int32, (NB, rank), 1)
    for b in range(rank // NB):
        s.a[NB * b:NB * (b + 1), rank:] = jnp.where(row + NB * b == lane, 1.0, 0.0).astype(F32)
    sum_round(half - 2)
    drain(s.gall.at[core, others(chips)], s.g_rs)
    across = send(s.gall.at[core], s.gall.at[core], s.e_ss, s.e_rs, col=partner)
    across.wait()
    for other in range(nc):
        for piece in range(nz):
            i, l = piece // glanes, piece % glanes
            top = other * share + tall * i
            s.a[top:top + tall, 128 * l:128 * l + 128] = s.gall[other % 2, other // 2, piece]

    sum_round(half - 4)

    blocks = rank // NB

    def step(b, carry):
        at = pl.multiple_of(b * NB, NB)
        s.d[...] = s.a[pl.ds(at, NB), pl.ds(at, NB)]
        diag_inverse(s.d, s.inv)
        for bb in range(blocks):
            @pl.when(b == bb)
            def _():
                low, top = bb * NB, (bb + 1) * NB
                prod = jnp.dot(s.inv[...], s.a[low:top, top:rank + top], precision=HI, preferred_element_type=F32)
                s.a[low:top, rank:rank + top] = prod[:, rank - top:]
                if bb < blocks - 1:
                    ut = prod[:, :rank - top].T
                    s.a[top:rank, top:rank + top] = s.a[top:rank, top:rank + top] - jnp.dot(
                        ut, prod, precision=HI, preferred_element_type=F32)
                if bb == 1:
                    for far in range(half - 6, 0, -2):
                        sum_round(far)
        return carry

    lax.fori_loop(0, blocks, step, 0)

    for chunk in (0, 1):
        value = share_of(z, chunk)[...]
        for way in (0, 1):
            value = value + inbound(s.leaf_came, s.l_rs, way, 0, chunk) + inbound(s.stem_came, s.r_rs, way, 0, chunk)
        s.own[chunk] = value
    right = sum(
        lax.dot_general(s.own[chunk], s.a[:, rank + hi * chunk:rank + hi * (chunk + 1)], NT,
                        precision=HI, preferred_element_type=F32)
        for chunk in (0, 1)
    )
    before = lax.rem(z + nz - 1, nz)
    seen = jnp.where(z == 0, 0, window_start(before, cols, nz) + win - window_start(z, cols, nz))
    fresh = lax.broadcasted_iota(jnp.int32, right.shape, 0) >= seen
    squares = jnp.sum(jnp.where(fresh, right * right, 0.0), axis=0, keepdims=True)
    for l in range(glanes):
        s.sz[z, l:l + 1, :] = squares[:, 128 * l:128 * l + 128]

    @pl.loop(1, nz)
    def _(j):
        send(s.sz.at[z], s.sz.at[z], s.n_ss, s.n_rs, row=lax.rem(z + j, nz))

    for chunk in (0, 1):
        s.right[0, chunk] = right[:, hi * chunk:hi * (chunk + 1)].astype(BF16)
    gather = Ring(s.right, s.p_ss, s.p_rs, z, nz)
    gather.round(0)

    p = jnp.dot(s.a[:, rank:], s.w[...], precision=HI, preferred_element_type=F32)
    s.plow[...] = p.astype(BF16)
    s.pt[...] = p.T
    out = p_out.shape[0]
    p_out[...] = s.pt[pl.ds(pl.multiple_of(c * out, out), out), :]

    for r in range(1, gather.rounds - 1):
        gather.round(r)
    drain(s.sz.at[others(nz)], s.n_rs)
    s.sx[c] = s.sz[...].sum(axis=0)

    @pl.loop(1, nc)
    def _(j):
        send(s.sx.at[c], s.sx.at[c], s.m_ss, s.m_rs, col=lax.rem(c + j, nc))

    gather.round(gather.rounds - 1)
    drain(s.sx.at[others(nc)], s.m_rs)
    total = s.sx[...].sum(axis=0)
    total = jnp.concatenate([total[l:l + 1, :] for l in range(glanes)], axis=1)
    pick = lax.broadcasted_iota(jnp.int32, (wide, rank), 1) == lax.broadcasted_iota(jnp.int32, (wide, rank), 0) + z * wide
    norms = jnp.sqrt(jnp.sum(jnp.where(pick, total, 0.0), axis=1, keepdims=True) + 1e-06)
    gather.slots_arrived(*range(nz))
    for slot in range(nz):
        at = window_start(lax.rem(z + nz - slot, nz), cols, nz)
        for chunk in (0, 1):
            s.r32[pl.ds(at, win), hi * chunk:hi * (chunk + 1)] = s.right[slot, chunk].astype(F32)
    low = s.r32[...].astype(BF16)
    update = jnp.dot(low, s.plow[...], preferred_element_type=F32)
    m_out[...] = (s.mom[...] + s.grad[...].astype(F32)) - 0.1 * update
    q_out[...] = lax.dot_general(jnp.where(pick, 1.0, 0.0).astype(BF16), low, NT, preferred_element_type=F32) / norms

    ring.finish()
    gather.finish()
    for p in range(half):
        drain(s.came.at[p, others(nc)], s.c_ss.at[p])
        if p in late:
            drain(s.came.at[p, others(nc)], s.a_ss.at[p])
        else:
            drain(s.shares.at[p, core, others(chips)], s.a_ss.at[p])
            drain(s.shares.at[p, core], s.d_ss.at[p])
    drain(s.gcame.at[others(nz)], s.z_ss)
    drain(s.grow.at[others(nz)], s.y_ss)
    drain(s.gall.at[core, others(chips)], s.g_ss)
    drain(s.sz.at[others(nz)], s.n_ss)
    drain(s.sx.at[others(nc)], s.m_ss)
    for way in (0, 1):
        for k in range(half // 2):
            for chunk in (0, 1):
                drain(s.leaf_came.at[way, k, chunk], s.l_ss.at[way, k, chunk])
                if k < half // 2 - 1 or chunk == way:
                    drain(s.stem_came.at[way, k, chunk], s.r_ss.at[way, k, chunk])


def run(mom, grad, q, nz, nc):
    cols, rows = mom.shape
    wide = q.shape[0]
    rank = wide * nz
    scratch = scratch_of(nz, nc, cols, rows, wide)
    names = list(scratch)
    whole = pl.BlockSpec(memory_space=pltpu.VMEM)
    return pl.pallas_call(
        lambda *refs: kernel(nz, nc, *refs[:6], SimpleNamespace(**dict(zip(names, refs[6:])))),
        out_shape=(
            jax.ShapeDtypeStruct((cols, rows), F32),
            jax.ShapeDtypeStruct((rows // nc, rank), F32),
            jax.ShapeDtypeStruct((wide, cols), F32),
        ),
        in_specs=[pl.BlockSpec(memory_space=pltpu.HBM)] * 3,
        out_specs=(whole,) * 3,
        scratch_shapes=list(scratch.values()),
        compiler_params=pltpu.CompilerParams(collective_id=0, has_side_effects=True, vmem_limit_bytes=67043328),
        name="dion",
    )(mom, grad, q)


def solution(mesh):
    nz, nc = mesh.shape["row"], mesh.shape["col"]

    def body(momentum, gradient, q_basis):
        mom_next, p_out, q_next = run(momentum.T, gradient.T, q_basis.T, nz, nc)
        return mom_next.T, p_out, q_next.T

    placed = (P("row", "col"), P("row", "col"), P("col", "row"))
    return jax.shard_map(
        body, mesh=mesh, in_specs=placed, out_specs=(P("row", "col"), P(("row", "col"), None), P("col", "row")),
        check_vma=False,
    )
```

time: 517 us -> 119 us (0.23); the launches traced: 510 us -> 118 us
  blocking collectives: 244 us -> 0 us
  other arithmetic: 122 us -> 0 us
  Pallas kernels: 0 us -> 113 us
  waiting for transfers between devices: 90.4 us -> 0 us
  matrix products: 22.1 us -> 0 us
  starting transfers between devices: 12 us -> 0 us
  local copies, waits for them, and re-layouts: 14.7 us -> 4.07 us
    all_to_all x7 -> x0, blocking collectives: 203 us -> none  [the longest x3 157 us: sum_at_owner(): lax.all_to_all(blocks, axis, split_axis=0, concat_axis=0, tiled=True)]
    another operation x18 -> x0, other arithmetic: 119 us -> none  [the longest x14 78.6 us: body(): lower = jnp.linalg.cholesky(gram)]
    pallas_call x0 -> x1, Pallas kernels: none -> 113 us  [run(): pl.pallas_call(lambda *refs: kernel(nz, nc, *refs[:6], SimpleNamespace(**...]
    all_to_all x2 -> x0, waiting for transfers between devices: 90.4 us -> none  [from_everyone(): return lax.all_to_all(copies, axis, split_axis=0, concat_axis=0, tiled=True)]
    all_gather x1 -> x0, blocking collectives: 40.9 us -> none  [body(): lax.all_gather(q_basis, 'row', axis=1, tiled=True)]
    another operation x13 -> x0, matrix products: 13.9 us -> none  [the longest x7 8.43 us: body(): p_full = jax.scipy.linalg.solve_triangular(lower, power.T, lower=True).T]
    all_to_all x2 -> x0, starting transfers between devices: 12 us -> none  [from_everyone(): return lax.all_to_all(copies, axis, split_axis=0, concat_axis=0, tiled=True)]
    dot_general x4 -> x0, matrix products: 8.2 us -> none  [the longest x1 3.12 us: body(): jnp.einsum('ir,cr->ic', p_low, right_low, preferred_element_type=jnp.floa...]
  transfers between devices with their start and end apart: 2 -> 0, of which waited for: 2 -> 0; matrix products, arithmetic and copies ran while one was open for 1% -> 0% of each run, Pallas kernels for 0% -> 0%
where the time goes in v3:
time: 119 us; the launch traced here: 118 us
  Pallas kernels  113 us (95%)
  local copies, waits for them, and re-layouts  4.07 us (3%)
    pallas_call x1, Pallas kernels, run(): pl.pallas_call(lambda *refs: kernel(nz, nc, *refs[:6], SimpleNamespace(**...  113 us
    unnamed x7, local copies, waits for them, and re-layouts  4.07 us

profile of v3, /device:TPU:24, one launch (start us, length us, event | category | flops | bytes accessed | tf_op | source)
XLA Modules:
  0.0 118.0 jit_solution(11100473985397238866)
XLA Ops:
  0.6 113.3 %dion.1 = (f32[832,512]{1,0:T(8,128)}, f32[16,512]{1,0:T(8,128)}, f32[32,832]{1,0:T(8,128)}) custom-call(f32[832,512]{1,0:T(8,128)} %bitcast.5, bf16[832,512]{1,0:T(8,128)(2,1)} %bitcast.7, bf16[32,832]{1,0:T(8,128)(2,1)} %bitcast.9), custom_call_target="tpu_custom_call" | custom-call | tf_op jit(solution)/shard_map/dion/pallas_call | solution.py:478
  113.9 0.0 copy-start.1
  113.9 0.0 copy-start
  114.0 2.8 %copy.9 = f32[512,832]{0,1:T(8,128)} copy(f32[512,832]{0,1:T(8,128)} %bitcast.6) | data formatting | bytes 3407872
  116.8 0.0 copy-done.1
  116.8 0.6 copy.10
  117.4 0.0 copy-done
  117.4 0.6 copy.11
Async XLA Ops:
  113.9 2.8 %copy-start.1 = (f32[16,512]{1,0:T(8,128)S(1)}, f32[16,512]{1,0:T(8,128)}, u32[]{:S(2)}) copy-start(f32[16,512]{1,0:T(8,128)} %get-tuple-element.13) | copy-start | bytes 98308
  113.9 3.4 %copy-start = (f32[32,832]{1,0:T(8,128)S(1)}, f32[32,832]{1,0:T(8,128)}, u32[]{:S(2)}) copy-start(f32[32,832]{1,0:T(8,128)} %get-tuple-element.8) | copy-start | bytes 319492

commit v4 on v3

--- a/solution.py
+++ b/solution.py
@@ -95,18 +95,20 @@
     lane = lax.broadcasted_iota(jnp.int32, (8, NB), 1)
     for g in range(n):
         inv_ref[8 * g:8 * g + 8, :] = jnp.where(row + 8 * g == lane, 1.0, 0.0).astype(jnp.float32)
+    rd, ri = d_ref[:8, :], inv_ref[:8, :]
+    c = [lane_bcast(rd, k) for k in range(8)]
     for s in range(n):
-        rd = d_ref[8 * s:8 * s + 8, :]
-        ri = inv_ref[8 * s:8 * s + 8, :]
-        c = [lane_bcast(rd, 8 * s + k) for k in range(8)]
+        follow = s + 1 < n
+        if follow:
+            rn, vn = d_ref[8 * s + 8:8 * s + 16, :], inv_ref[8 * s + 8:8 * s + 16, :]
+            ca = [lane_bcast(rn, 8 * s + k) for k in range(8)]
+            cb = [lane_bcast(rn, 8 * s + 8 + k) for k in range(8)]
         u = {}
-        scale = []
-        ud = []
-        ui = []
+        scale, ud, ui = [], [], []
         for j in range(8):
             rs = lax.rsqrt(sub_bcast(c[j], j))
             scale.append(rs)
-            lj = jnp.where(row > j, c[j] * rs, 0.0)
+            lj = jnp.where(row > j, c[j], 0.0) * rs
             for k in range(j + 1, 8):
                 u[j, k] = sub_bcast(c[k], j) * rs
                 c[k] = c[k] - lj * u[j, k]
@@ -114,22 +116,32 @@
             ui.append(sub_bcast(ri, j) * rs)
             rd = rd - lj * ud[j]
             ri = ri - lj * ui[j]
+            if follow:
+                ln = ca[j] * rs
+                for k in range(j + 1, 8):
+                    ca[k] = ca[k] - ln * u[j, k]
+                for k in range(8):
+                    cb[k] = cb[k] - ln * sub_bcast(ln, k)
+                rn = rn - ln * ud[j]
+                vn = vn - ln * ui[j]
         out = ui[7]
         for j in range(7):
             out = jnp.where(row == j, ui[j], out)
         inv_ref[8 * s:8 * s + 8, :] = out
-        for g in range(s + 1, n):
-            rd = d_ref[8 * g:8 * g + 8, :]
-            ri = inv_ref[8 * g:8 * g + 8, :]
-            c = [lane_bcast(rd, 8 * s + k) for k in range(8)]
+        for g in range(s + 2, n):
+            rg = d_ref[8 * g:8 * g + 8, :]
+            vg = inv_ref[8 * g:8 * g + 8, :]
+            cg = [lane_bcast(rg, 8 * s + k) for k in range(8)]
             for j in range(8):
-                lj = c[j] * scale[j]
+                lg = cg[j] * scale[j]
                 for k in range(j + 1, 8):
-                    c[k] = c[k] - lj * u[j, k]
-                rd = rd - lj * ud[j]
-                ri = ri - lj * ui[j]
-            d_ref[8 * g:8 * g + 8, :] = rd
-            inv_ref[8 * g:8 * g + 8, :] = ri
+                    cg[k] = cg[k] - lg * u[j, k]
+                rg = rg - lg * ud[j]
+                vg = vg - lg * ui[j]
+            d_ref[8 * g:8 * g + 8, :] = rg
+            inv_ref[8 * g:8 * g + 8, :] = vg
+        if follow:
+            c, rd, ri = cb, rn, vn
 
 
 def scratch_of(nz, nc, cols, rows, wide):
@@ -141,7 +153,7 @@
     return dict(
         mom=vm((cols, rows), F32), grad=vm((cols, rows), BF16), blow=vm((cols, rows), BF16),
         held=vm((nz, 2, thin, cols), BF16),
-        parts=vm((half, 2, chips, 8, 128), F32), came=vm((half, nc, 8, 128), F32),
+        parts=vm((half, 2, chips, 8, 128), F32), mate=vm((half, chips, 8, 128), F32), came=vm((half, nc, 8, 128), F32),
         shares=vm((half, 2, chips, 8, 128), F32), w=vm((rank, rows), F32),
         gpart=vm((nz, tall, 128), F32), gcame=vm((nz, tall, 128), F32), grow=vm((nz, tall, 128), F32),
         gall=vm((2, chips, nz, tall, 128), F32),
@@ -149,11 +161,11 @@
         y=vm((2, cols, hi), F32),
         leaf_came=vm((2, quarter, 2, win, hi), F32), stem=vm((2, quarter, 2, win, hi), F32),
         stem_came=vm((2, quarter, 2, win, hi), F32), own=vm((2, win, hi), F32),
-        right=vm((nz, 2, win, hi), BF16), r32=vm((cols, rank), F32),
+        right=vm((nz, 2, win * (hi // 128), 128), BF16), r32=vm((cols, rank), F32),
         plow=vm((rank, rows), BF16), pt=vm((rows, rank), F32),
         sz=vm((nz, rank // 128, 128), F32), sx=vm((nc, rank // 128, 128), F32),
         q_ss=DMA((2, quarter, 2, 2)), q_rs=DMA((nz, 2)),
-        c_ss=DMA((half,)), c_rs=DMA((half,)), a_ss=DMA((half,)), a_rs=DMA((half,)), d_ss=DMA((half,)), d_rs=DMA((half,)),
+        b_ss=DMA((half,)), b_rs=DMA((half,)), c_ss=DMA((half,)), c_rs=DMA((half,)), a_ss=DMA((half,)), a_rs=DMA((half,)), d_ss=DMA((half,)), d_rs=DMA((half,)),
         z_ss=DMA, z_rs=DMA, y_ss=DMA, y_rs=DMA, g_ss=DMA, g_rs=DMA, e_ss=DMA, e_rs=DMA,
         l_ss=DMA((2, quarter, 2)), l_rs=DMA((2, quarter, 2)), r_ss=DMA((2, quarter, 2)), r_rs=DMA((2, quarter, 2)),
         p_ss=DMA((2, quarter, 2, 2)), p_rs=DMA((nz, 2)),
@@ -217,22 +229,29 @@
         prod = jnp.dot(lhs, s.blow[...], preferred_element_type=F32)
         for i, p in enumerate(pairs):
             pass_on(p, prod[2 * wide * i:2 * wide * (i + 1)])
+        for p in pairs:
+            merge(p)
 
     def pass_on(p, prod):
         for side in (0, 1):
             for piece in range(chips):
                 i, l = piece // lanes, piece % lanes
                 s.parts[p, side, piece] = prod[side * wide + 8 * i:side * wide + 8 * i + 8, 128 * l:128 * l + 128]
-        s.came[p, c] = s.parts[p, core, chip]
-
-        @pl.loop(1, nc)
+        send(s.parts.at[p, 1 - core], s.mate.at[p], s.b_ss.at[p], s.b_rs.at[p], col=partner)
+
+    def merge(p):
+        drain(s.mate.at[p], s.b_rs.at[p])
+        s.parts[p, core] = s.parts[p, core] + s.mate[p]
+        s.came[p, chip] = s.parts[p, core, chip]
+
+        @pl.loop(1, chips)
         def _(j):
-            to = lax.rem(c + j, nc)
-            send(s.parts.at[p, lax.rem(to, 2), lax.div(to, 2)], s.came.at[p, c], s.c_ss.at[p], s.c_rs.at[p], col=to)
+            other = lax.rem(chip + j, chips)
+            send(s.parts.at[p, core, other], s.came.at[p, chip], s.c_ss.at[p], s.c_rs.at[p], col=other * 2 + core)
 
     def add_up(p):
-        drain(s.came.at[p, others(nc)], s.c_rs.at[p])
-        s.shares[p, core, chip] = s.came[p].sum(axis=0)
+        drain(s.came.at[p, others(chips)], s.c_rs.at[p])
+        s.shares[p, core, chip] = s.came[p, pl.ds(0, chips)].sum(axis=0)
         mine = s.shares.at[p, core, chip]
         if p in late:
             @pl.loop(1, nc)
@@ -411,7 +430,8 @@
         send(s.sz.at[z], s.sz.at[z], s.n_ss, s.n_rs, row=lax.rem(z + j, nz))
 
     for chunk in (0, 1):
-        s.right[0, chunk] = right[:, hi * chunk:hi * (chunk + 1)].astype(BF16)
+        strips = [right[:, hi * chunk + 128 * l:hi * chunk + 128 * (l + 1)] for l in range(hi // 128)]
+        s.right[0, chunk] = jnp.concatenate(strips, axis=0).astype(BF16)
     gather = Ring(s.right, s.p_ss, s.p_rs, z, nz)
     gather.round(0)
 
@@ -440,16 +460,20 @@
     for slot in range(nz):
         at = window_start(lax.rem(z + nz - slot, nz), cols, nz)
         for chunk in (0, 1):
-            s.r32[pl.ds(at, win), hi * chunk:hi * (chunk + 1)] = s.right[slot, chunk].astype(F32)
+            strips = s.right[slot, chunk].astype(F32)
+            for l in range(hi // 128):
+                left = hi * chunk + 128 * l
+                s.r32[pl.ds(at, win), left:left + 128] = strips[win * l:win * (l + 1)]
     low = s.r32[...].astype(BF16)
     update = jnp.dot(low, s.plow[...], preferred_element_type=F32)
-    m_out[...] = (s.mom[...] + s.grad[...].astype(F32)) - 0.1 * update
+    m_out[...] = (0.1 * update).astype(BF16)
     q_out[...] = lax.dot_general(jnp.where(pick, 1.0, 0.0).astype(BF16), low, NT, preferred_element_type=F32) / norms
 
     ring.finish()
     gather.finish()
     for p in range(half):
-        drain(s.came.at[p, others(nc)], s.c_ss.at[p])
+        drain(s.mate.at[p], s.b_ss.at[p])
+        drain(s.came.at[p, others(chips)], s.c_ss.at[p])
         if p in late:
             drain(s.came.at[p, others(nc)], s.a_ss.at[p])
         else:
@@ -478,7 +502,7 @@
     return pl.pallas_call(
         lambda *refs: kernel(nz, nc, *refs[:6], SimpleNamespace(**dict(zip(names, refs[6:])))),
         out_shape=(
-            jax.ShapeDtypeStruct((cols, rows), F32),
+            jax.ShapeDtypeStruct((cols, rows), BF16),
             jax.ShapeDtypeStruct((rows // nc, rank), F32),
             jax.ShapeDtypeStruct((wide, cols), F32),
         ),
@@ -494,8 +518,9 @@
     nz, nc = mesh.shape["row"], mesh.shape["col"]
 
     def body(momentum, gradient, q_basis):
-        mom_next, p_out, q_next = run(momentum.T, gradient.T, q_basis.T, nz, nc)
-        return mom_next.T, p_out, q_next.T
+        change, p_out, q_next = run(momentum.T, gradient.T, q_basis.T, nz, nc)
+        mom_next = (momentum + gradient.astype(F32)) - change.T.astype(F32)
+        return mom_next, p_out, q_next.T
 
     placed = (P("row", "col"), P("row", "col"), P("col", "row"))
     return jax.shard_map(

time: 119 us -> 117 us (0.983)
  other arithmetic: 0 us -> 3.49 us
  local copies, waits for them, and re-layouts: 4.07 us -> 1.27 us
  Pallas kernels: 113 us -> 111 us
    sub x0 -> x1, other arithmetic: none -> 3.49 us  [body(): mom_next = momentum + gradient.astype(F32) - change.T.astype(F32)]
    unnamed x7 -> x6, local copies, waits for them, and re-layouts: 4.07 us -> 1.27 us
    pallas_call x1, Pallas kernels: 113 us -> 111 us  [run(): pl.pallas_call(lambda *refs: kernel(nz, nc, *refs[:6], SimpleNamespace(**...]
where the time goes in v4:
time: 117 us
  Pallas kernels  111 us (95%)
  other arithmetic  3.49 us (3%)
  local copies, waits for them, and re-layouts  1.27 us (1%)
    pallas_call x1, Pallas kernels, run(): pl.pallas_call(lambda *refs: kernel(nz, nc, *refs[:6], SimpleNamespace(**...  111 us
    sub x1, other arithmetic, body(): mom_next = momentum + gradient.astype(F32) - change.T.astype(F32)  3.49 us

profile of v4, /device:TPU:24, one launch (start us, length us, event | category | flops | bytes accessed | tf_op | source)
XLA Modules:
  0.0 116.8 jit_solution(12107312890073942185)
XLA Ops:
  0.6 111.4 %dion.1 = (bf16[832,512]{1,0:T(8,128)(2,1)}, f32[16,512]{1,0:T(8,128)}, f32[32,832]{1,0:T(8,128)}) custom-call(f32[832,512]{1,0:T(8,128)} %bitcast.6, bf16[832,512]{1,0:T(8,128)(2,1)} %bitcast.7, bf16[32,832]{1,0:T(8,128)(2,1)} %bitcast.9), custom_call_target="tpu_custom_call" | custom-call | tf_op jit(solution)/shard_map/dion/pallas_call | solution.py:502
  112.0 0.0 copy-start.1
  112.0 0.0 copy-start
  112.1 3.5 %bitcast_subtract_fusion = f32[512,832]{0,1:T(8,128)} fusion(bf16[832,512]{1,0:T(8,128)(2,1)} %get-tuple-element.6, f32[512,832]{0,1:T(8,128)} %param.3, bf16[512,832]{0,1:T(8,128)(2,1)} %param.4), kind=kLoop, calls=%fused_computation | loop fusion | flops 1703936 | bytes 5111808 | tf_op jit(solution)/shard_map/sub | solution.py:522
  115.6 0.0 copy-done.1
  115.6 0.6 copy.8
  116.2 0.0 copy-done
  116.2 0.6 copy.9
Async XLA Ops:
  112.0 3.5 %copy-start.1 = (f32[16,512]{1,0:T(8,128)S(1)}, f32[16,512]{1,0:T(8,128)}, u32[]{:S(2)}) copy-start(f32[16,512]{1,0:T(8,128)} %get-tuple-element.13) | copy-start | bytes 98308
  112.0 4.1 %copy-start = (f32[32,832]{1,0:T(8,128)S(1)}, f32[32,832]{1,0:T(8,128)}, u32[]{:S(2)}) copy-start(f32[32,832]{1,0:T(8,128)} %get-tuple-element.8) | copy-start | bytes 319492

commit v5 on v4

--- a/solution.py
+++ b/solution.py
@@ -466,7 +466,7 @@
                 s.r32[pl.ds(at, win), left:left + 128] = strips[win * l:win * (l + 1)]
     low = s.r32[...].astype(BF16)
     update = jnp.dot(low, s.plow[...], preferred_element_type=F32)
-    m_out[...] = (0.1 * update).astype(BF16)
+    m_out[...] = (s.mom[...] + s.grad[...].astype(F32)) - 0.1 * update
     q_out[...] = lax.dot_general(jnp.where(pick, 1.0, 0.0).astype(BF16), low, NT, preferred_element_type=F32) / norms
 
     ring.finish()
@@ -502,25 +502,24 @@
     return pl.pallas_call(
         lambda *refs: kernel(nz, nc, *refs[:6], SimpleNamespace(**dict(zip(names, refs[6:])))),
         out_shape=(
-            jax.ShapeDtypeStruct((cols, rows), BF16),
+            jax.ShapeDtypeStruct((cols, rows), F32),
             jax.ShapeDtypeStruct((rows // nc, rank), F32),
             jax.ShapeDtypeStruct((wide, cols), F32),
         ),
         in_specs=[pl.BlockSpec(memory_space=pltpu.HBM)] * 3,
         out_specs=(whole,) * 3,
         scratch_shapes=list(scratch.values()),
-        compiler_params=pltpu.CompilerParams(collective_id=0, has_side_effects=True, vmem_limit_bytes=67043328),
+        compiler_params=pltpu.CompilerParams(collective_id=0, has_side_effects=True, vmem_limit_bytes=40 * 1024 * 1024),
         name="dion",
-    )(mom, grad, q)
+    )(*(pltpu.with_memory_space_constraint(x, pltpu.HBM) for x in (mom, grad, q)))
 
 
 def solution(mesh):
     nz, nc = mesh.shape["row"], mesh.shape["col"]
 
     def body(momentum, gradient, q_basis):
-        change, p_out, q_next = run(momentum.T, gradient.T, q_basis.T, nz, nc)
-        mom_next = (momentum + gradient.astype(F32)) - change.T.astype(F32)
-        return mom_next, p_out, q_next.T
+        mom_next, p_out, q_next = run(momentum.T, gradient.T, q_basis.T, nz, nc)
+        return mom_next.T, p_out, q_next.T
 
     placed = (P("row", "col"), P("row", "col"), P("col", "row"))
     return jax.shard_map(

time: 117 us -> 114 us (0.974)
  other arithmetic: 3.49 us -> 0 us
  local copies, waits for them, and re-layouts: 1.27 us -> 2.45 us
    sub x1 -> x0, other arithmetic: 3.49 us -> none  [body(): mom_next = momentum + gradient.astype(F32) - change.T.astype(F32)]
    unnamed x6 -> x3, local copies, waits for them, and re-layouts: 1.27 us -> 2.45 us
where the time goes in v5:
time: 114 us
  Pallas kernels  111 us (97%)
  local copies, waits for them, and re-layouts  2.45 us (2%)
    pallas_call x1, Pallas kernels, run(): pl.pallas_call(lambda *refs: kernel(nz, nc, *refs[:6], SimpleNamespace(**...  111 us
    unnamed x3, local copies, waits for them, and re-layouts  2.45 us

profile of v5, /device:TPU:24, one launch (start us, length us, event | category | flops | bytes accessed | tf_op | source)
XLA Modules:
  0.0 114.1 jit_solution(12579303136845293727)
XLA Ops:
  0.6 111.0 %dion.1 = (f32[832,512]{1,0:T(8,128)S(1)}, f32[16,512]{1,0:T(8,128)S(1)}, f32[32,832]{1,0:T(8,128)S(1)}) custom-call(f32[832,512]{1,0:T(8,128)} %bitcast.7, bf16[832,512]{1,0:T(8,128)(2,1)} %bitcast.8, bf16[32,832]{1,0:T(8,128)(2,1)} %bitcast.9), custom_call_target="tpu_custom_call" | custom-call | tf_op jit(solution)/shard_map/dion/pallas_call | solution.py:502
  111.6 1.2 %copy.9 = f32[512,832]{0,1:T(8,128)} copy(f32[512,832]{0,1:T(8,128)S(1)} %bitcast.5) | data formatting | bytes 3407872
  112.8 0.6 copy.10
  113.4 0.6 copy.11
